TPU v7x, 8 devices: a whole 2x2x1 slice. The times are simulated.
8 devices in a mesh: data: 1 (over z), chip: 2 (over y), dap: 4 (over x, core).
Axes of the slice: x: 2, y: 2, z: 1, core: 2. Of those that a mesh axis runs over, the one named last changes fastest.
Arguments:
- m: bfloat16 [256, 96, 256], P(('data', 'chip', 'dap'))
- z: bfloat16 [96, 96, 128], P(('data', 'chip', 'dap'))
- msa_mask: int32 [256, 96], P('data')
- res_mask: int32 [96], P('data')
- w_row_in: bfloat16 [256, 1024], replicated
- w_row_bias: bfloat16 [128, 8], replicated
- w_row_out: bfloat16 [256, 256], replicated
- w_col_in: bfloat16 [256, 1024], replicated
- w_col_out: bfloat16 [256, 256], replicated
- w_opm_in: bfloat16 [256, 64], replicated
- w_opm_out: bfloat16 [1024, 128], replicated
- w_start_in: bfloat16 [128, 512], replicated
- w_start_bias: bfloat16 [128, 4], replicated
- w_start_out: bfloat16 [128, 128], replicated
- w_end_in: bfloat16 [128, 512], replicated
- w_end_bias: bfloat16 [128, 4], replicated
- w_end_out: bfloat16 [128, 128], replicated
Outputs:
- output 1: bfloat16 [256, 96, 256], P(('data', 'chip', 'dap'))
- output 2: bfloat16 [96, 96, 128], P(('data', 'chip', 'dap'))
All inputs are finite; a program needn't handle non-finite values.
Results may differ from a plain program's by a relative error of at most 0.0151752.
Values are sent between devices in bfloat16 or wider.
A program may use at most 1 GiB of HBM per device.

v0:
```python
import jax
import jax.numpy as jnp
from jax import lax
from jax.sharding import PartitionSpec as P


def layer_norm(x):
    values = x.astype(jnp.float32)
    centred = values - jnp.mean(values, axis=-1, keepdims=True)
    variance = jnp.mean(centred * centred, axis=-1, keepdims=True)
    return (centred * lax.rsqrt(variance + 1e-5)).astype(jnp.bfloat16)


def add_residual(state, update):
    return (state.astype(jnp.float32) + update).astype(jnp.bfloat16)


def gated_attention(x_norm, w_in, w_out, heads, head_bias, key_ok, along_first):
    width = x_norm.shape[-1]
    head_dim = w_out.shape[0] // heads
    w_heads = jnp.transpose(w_in.reshape(width, 4, heads, head_dim), (2, 0, 1, 3))
    w_back = w_out.reshape(heads, head_dim, w_out.shape[1])
    if along_first:
        forms = ('nbc,cfd->nbfd', 'ibd,jbd->bij', 'bij,jbd->ibd', 'hibd,hdc->ibc')
    else:
        forms = ('bnc,cfd->bnfd', 'bid,bjd->bij', 'bij,bjd->bid', 'hbid,hdc->bic')
    key_keep = key_ok[:, None, :]
    scale = head_dim ** -0.5

    def one_head(head_in):
        projected = jnp.einsum(forms[0], x_norm, head_in[0], preferred_element_type=jnp.float32).astype(jnp.bfloat16)
        scores = jnp.einsum(forms[1], projected[:, :, 0], projected[:, :, 1], preferred_element_type=jnp.float32) * scale
        if len(head_in) > 1:
            scores = scores + head_in[1].astype(jnp.float32)[None]
        scores = jnp.where(key_keep, scores, -1e9)
        attn_prob = jax.nn.softmax(scores, axis=-1).astype(jnp.bfloat16)
        mixed = jnp.einsum(forms[2], attn_prob, projected[:, :, 2], preferred_element_type=jnp.float32)
        return (mixed * jax.nn.sigmoid(projected[:, :, 3].astype(jnp.float32))).astype(jnp.bfloat16)

    head_in = (w_heads,) if head_bias is None else (w_heads, head_bias)
    gated = lax.map(one_head, head_in)
    return jnp.einsum(forms[3], gated, w_back, preferred_element_type=jnp.float32)


def solution(mesh):
    dap_size = mesh.shape['dap']
    group = ('chip', 'dap')
    rows = P(('data', 'chip', 'dap'))
    in_specs = (rows, rows, P('data'), P('data')) + (P(),) * 13

    def per_device(m_blk, z_blk, value_a8, res_mask, w_row_in, w_row_bias, w_row_out, w_col_in, w_col_out,
                   w_opm_in, w_opm_out, w_start_in, w_start_bias, w_start_out, w_end_in, w_end_bias, w_end_out):
        group_idx = lax.axis_index('chip') * dap_size + lax.axis_index('dap')
        seq_loc = m_blk.shape[0]
        res_loc = z_blk.shape[0]
        heads_m = w_row_bias.shape[1]
        heads_t = w_start_bias.shape[1]
        opm = w_opm_in.shape[1] // 2
        value_a6 = value_a8 != 0
        res_ok = (res_mask != 0)[None, :]

        row_bias = jnp.einsum('ijc,ch->hij', layer_norm(z_blk), w_row_bias, preferred_element_type=jnp.float32).astype(jnp.bfloat16)
        row_bias = lax.all_gather(row_bias, group, axis=1, tiled=True)
        seq_ok = lax.dynamic_slice_in_dim(value_a6, group_idx * seq_loc, seq_loc, axis=0)
        m_blk = add_residual(m_blk, gated_attention(layer_norm(m_blk), w_row_in, w_row_out, heads_m, row_bias, seq_ok, False))

        m_cols = lax.all_to_all(m_blk, group, 1, 0, tiled=True)
        col_mask = lax.dynamic_slice_in_dim(value_a8, group_idx * res_loc, res_loc, axis=1)
        m_cols = add_residual(m_cols, gated_attention(layer_norm(m_cols), w_col_in, w_col_out, heads_m, None, (col_mask != 0).T, True))

        outer_proj = jnp.dot(layer_norm(m_cols), w_opm_in, preferred_element_type=jnp.float32).astype(jnp.bfloat16)
        col_w = col_mask.astype(jnp.bfloat16)
        left = outer_proj[:, :, :opm] * col_w[:, :, None]
        right = lax.all_gather(outer_proj[:, :, opm:] * col_w[:, :, None], group, axis=1, tiled=True)
        pair_norm = jnp.einsum('si,sj->ij', col_w, value_a8.astype(jnp.bfloat16), preferred_element_type=jnp.float32)
        outer = jnp.einsum('sia,sjc->ijac', left, right, preferred_element_type=jnp.float32).astype(jnp.bfloat16)
        outer = outer.reshape(res_loc, outer.shape[1], opm * opm)
        z_blk = add_residual(z_blk, jnp.dot(outer, w_opm_out, preferred_element_type=jnp.float32) / (1e-3 + pair_norm[:, :, None]))

        start_norm = layer_norm(z_blk)
        start_bias = jnp.einsum('jkc,ch->hjk', start_norm, w_start_bias, preferred_element_type=jnp.float32).astype(jnp.bfloat16)
        start_bias = lax.all_gather(start_bias, group, axis=1, tiled=True)
        z_blk = add_residual(z_blk, gated_attention(start_norm, w_start_in, w_start_out, heads_t, start_bias, res_ok, False))

        z_cols = lax.all_to_all(z_blk, group, 1, 0, tiled=True)
        end_norm = layer_norm(z_cols)
        end_bias = jnp.einsum('kjc,ch->hjk', end_norm, w_end_bias, preferred_element_type=jnp.float32).astype(jnp.bfloat16)
        end_bias = lax.all_gather(end_bias, group, axis=1, tiled=True)
        z_cols = add_residual(z_cols, gated_attention(end_norm, w_end_in, w_end_out, heads_t, end_bias, res_ok, True))

        z_out = lax.all_to_all(z_cols, group, 0, 1, tiled=True)
        m_out = lax.all_to_all(m_cols, group, 0, 1, tiled=True)
        return m_out, z_out

    return jax.shard_map(per_device, mesh=mesh, in_specs=in_specs, out_specs=(rows, rows), check_vma=False)
```

profile of v0, /device:TPU:0, one launch (start us, length us, event | category | flops | bytes accessed | tf_op | source)
XLA Modules:
  0.0 306.0 jit_solution(15162396102826065227)
XLA Ops:
  13.6 14.1 %all_gather.12 = bf16[8,96,96]{2,0,1:T(8,128)(2,1)S(1)} all-gather(bf16[8,12,96]{2,0,1:T(8,128)(2,1)S(1)} %fusion.108), channel_id=1, replica_groups=mesh['data'=1,'chip'=2,'dap'=4] {'chip','dap'}, dimensions={1}, use_global_device_ids=true | all-gather | bytes 165888 | tf_op jit(solution)/shard_map/all_gather | solution.py:63
  28.8 47.1 %while.40 = (s32[]{:T(128)}, bf16[8,32,96,32]{2,3,1,0:T(8,128)(2,1)}, pred[32,1,96]{2,0,1:T(8,128)(4,1)S(1)}, bf16[8,256,4,32]{1,3,0,2:T(8,128)(2,1)S(1)}, bf16[...) while((s32[]{:T(128)}, bf16[8,32,96,32]{2,3,1,0:T(8,128)(2,1)}, ...), condition=%wide.region_7.8_spmd, body=%wide.region_4.7_spmd.sunk | while | flops 242132064 | bytes 6625877 | solution.py:41
  32.3 2.4 fusion.174
  38.1 2.4 fusion.174
  44.0 2.4 fusion.174
  49.9 2.5 fusion.174
  55.8 2.5 fusion.174
  61.7 2.5 fusion.174
  67.6 2.4 fusion.174
  73.5 2.5 fusion.174
  75.9 2.9 fusion.90
  80.9 2.4 all-to-all-start
  83.9 20.4 %all-to-all-done = bf16[32,96,256]{2,0,1:T(8,128)(2,1)S(1)} async-done(((bf16[32,96,256]{2,0,1:T(8,128)(2,1)}), bf16[32,96,256]{2,0,1:T(8,128)(2,1)S(1)}, u32[]{:S(2)}, u32[]{:S(2)}) %all-to-all-start) | async-done | bytes 1572896 | tf_op jit(solution)/shard_map/all_to_all | solution.py:67
  108.0 4.0 %copy.140 = f32[8,32,12,256]{3,1,0,2:T(8,128)} copy(f32[8,32,12,256]{3,1,2,0:T(8,128)} %convert_bitcast_fusion.1) | data formatting | bytes 6291456 | tf_op jit(solution)/shard_map/convert_element_type | solution.py:15
  112.0 2.4 multiply_convert_fusion
  114.5 49.9 %while.41 = (s32[]{:T(128)}, bf16[8,256,12,32]{1,3,2,0:T(8,128)(2,1)}, bf16[8,256,4,32]{1,3,0,2:T(8,128)(2,1)S(1)}, bf16[256,12,256]{2,0,1:T(8,128)(2,1)S(1)}, pred[12,1,256]{2,0,1:T(8,128)(4,1)S(1)}, /*index=5*/s32[]{:T(128)}) while((s32[]{:T(128)}, bf16[8,256,12,32]{1,3,2,0:T(8,128)(2,1)}, bf16[8,256,4,32]{1,3,0,2:T(8,128)(2,1)S(1)}, ...), condition=%wide.region_13.14_spmd, body=%wide.region_10.13_spmd.sunk | while | flops 307691776 | bytes 9732681 | solution.py:41
  115.1 2.6 fusion.178
  117.7 3.0 fusion.179
  121.4 2.6 fusion.178
  124.0 3.0 fusion.179
  127.6 2.6 fusion.178
  130.2 3.0 fusion.179
  133.8 2.6 fusion.178
  136.4 3.0 fusion.179
  140.0 2.6 fusion.178
  142.6 3.0 fusion.179
  146.3 2.6 fusion.178
  148.9 3.0 fusion.179
  152.5 2.6 fusion.178
  155.1 3.0 fusion.179
  158.7 2.6 fusion.178
  161.3 3.0 fusion.179
  164.3 3.7 %copy.145 = f32[256,12,256]{0,2,1:T(8,128)} copy(f32[256,12,256]{2,0,1:T(8,128)} %bitcast.427) | data formatting | bytes 6291456 | tf_op jit(solution)/shard_map/convert_element_type | solution.py:15
  168.0 2.6 convert_reduce_fusion.1
  172.8 18.7 %all-gather.2.cloned.1.call-done = bf16[256,96,32]{0,2,1:T(8,128)(2,1)} async-done(((bf16[256,12,32]{0,2,1:T(8,128)(2,1)}), bf16[256,96,32]{0,2,1:T(8,128)(2,1)}) %all-gather.2.cloned.1.call-update) | async-done | bytes 1572880 | tf_op jit(solution)/shard_map/all_gather | solution.py:74
  191.4 6.5 %convert_bitcast_fusion = bf16[12,96,32,32]{2,3,0,1:T(8,128)(2,1)} fusion(bf16[256,96,32]{0,2,1:T(8,128)(2,1)} %all-gather.2.cloned.1.call-done, bf16[256,12,64]{0,2,1:T(8,128)(2,1)S(1)} %fusion.99, bf16[256,12]{0,1:T(8,128)(2,1)S(1)} %dynamic-slice_convert_fusion), kind=kOutput, calls=%fused_computation.102 | convolution fusion | flops 605552640 | bytes 4136960 | tf_op jit(solution)/shard_map/sia,sjc->ijac/dot_general | solution.py:76
  197.9 12.1 %copy.150 = bf16[12,96,32,32]{1,3,2,0:T(8,128)(2,1)} copy(bf16[12,96,32,32]{2,3,0,1:T(8,128)(2,1)} %convert_bitcast_fusion) | data formatting | bytes 4718592 | tf_op jit(solution)/shard_map/convert_element_type | solution.py:76
  210.0 3.2 %fusion.131 = (f32[12,96]{1,0:T(8,128)S(1)}, f32[12,96,128]{2,1,0:T(8,128)S(1)}) fusion(f32[12,96]{1,0:T(8,128)S(1)} %convolution_add_fusion, bf16[12,96,1024]{1,2,0:T(8,128)(2,1)} %bitcast.433, bf16[1024,128]{1,0:T(8,128)(2,1)S(1)} %copy-done, bf16[12,96,128]{2,1,0:T(8,128)(2,1)S(1)} %copy-done.5), kind=kOutput, calls=%fused_computation.189 | convolution fusion | flops 302873472 | bytes 3515392 | tf_op jit(solution)/shard_map/dot_general | solution.py:78
  214.7 11.3 %all_gather.14 = bf16[4,96,96]{2,0,1:T(4,128)(2,1)S(1)} all-gather(bf16[4,12,96]{2,0,1:T(4,128)(2,1)S(1)} %fusion.109), channel_id=1, replica_groups=mesh['data'=1,'chip'=2,'dap'=4] {'chip','dap'}, dimensions={1}, use_global_device_ids=true | all-gather | bytes 82944 | tf_op jit(solution)/shard_map/all_gather | solution.py:82
  226.1 8.2 %while.42 = (s32[]{:T(128)}, bf16[4,12,96,32]{2,3,1,0:T(8,128)(2,1)}, pred[1,1,96]{2,1,0:T(4,128)(4,1)S(1)}, bf16[4,128,4,32]{1,3,0,2:T(8,128)(2,1)S(1)}, bf16[1...) while((s32[]{:T(128)}, bf16[4,12,96,32]{2,3,1,0:T(8,128)(2,1)}, ...), condition=%wide.region_21.22_spmd, body=%wide.region_18.21_spmd.sunk | while | flops 60578112 | bytes 3100757 | solution.py:41
  236.7 2.2 all-to-all-start.2
  239.0 3.0 copy.146
  242.0 4.8 %all-to-all-done.2 = bf16[12,96,128]{2,0,1:T(8,128)(2,1)S(1)} async-done(((bf16[12,96,128]{2,0,1:T(8,128)(2,1)}), bf16[12,96,128]{2,0,1:T(8,128)(2,1)S(1)}, u32[]{:S(2)}, u32[]{:S(2)}) %all-to-all-start.2) | async-done | bytes 294944 | tf_op jit(solution)/shard_map/all_to_all | solution.py:85
  246.9 3.1 %all-to-all-start.1 = ((bf16[256,12,256]{2,1,0:T(8,128)(2,1)}), bf16[256,12,256]{2,1,0:T(8,128)(2,1)}, u32[]{:S(2)}, u32[]{:S(2)}) async-start(bf16[256,12,256]{2,1,0:T(8,128)(2,1)} %copy.146), calls=%async_computation.1 | async-start | bytes 4194304 | tf_op jit(solution)/shard_map/all_to_all | solution.py:92
  252.5 28.6 %all_gather.15 = bf16[4,96,96]{2,0,1:T(4,128)(2,1)S(1)} all-gather(bf16[4,12,96]{2,0,1:T(4,128)(2,1)S(1)} %fusion.110), channel_id=1, replica_groups=mesh['data'=1,'chip'=2,'dap'=4] {'chip','dap'}, dimensions={1}, use_global_device_ids=true | all-gather | bytes 82944 | tf_op jit(solution)/shard_map/all_gather | solution.py:88
  281.2 5.7 %while.43 = (s32[]{:T(128)}, bf16[4,96,12,32]{1,3,2,0:T(8,128)(2,1)S(1)}, bf16[4,128,4,32]{1,3,0,2:T(8,128)(2,1)S(1)}, bf16[96,12,128]{2,0,1:T(8,128)(2,1)S(1)},...) while((s32[]{:T(128)}, bf16[4,96,12,32]{1,3,2,0:T(8,128)(2,1)S(1)}, ...), condition=%wide.region_27.28_spmd, body=%wide.region_24.27_spmd.sunk | while | flops 60578112 | bytes 2752601 | solution.py:41
  288.1 2.2 all-to-all-start.3
  294.5 3.8 %all-to-all-done.3 = bf16[96,12,128]{2,1,0:T(8,128)(2,1)S(1)} async-done(((bf16[96,12,128]{2,1,0:T(8,128)(2,1)}), bf16[96,12,128]{2,1,0:T(8,128)(2,1)S(1)}, u32[]{:S(2)}, u32[]{:S(2)}) %all-to-all-start.3) | async-done | bytes 294944 | tf_op jit(solution)/shard_map/all_to_all | solution.py:91
  (180 shorter events, 74.6 us)
Async XLA Ops:
  7.2 202.9 %copy-start = (bf16[1024,128]{1,0:T(8,128)(2,1)S(1)}, bf16[1024,128]{1,0:T(8,128)(2,1)}, u32[]{:S(2)}) copy-start(bf16[1024,128]{1,0:T(8,128)(2,1)} %param.35) | copy-start | bytes 786436
  7.2 3.2 %copy-start.1 = (bf16[32,96,256]{2,1,0:T(8,128)(2,1)S(1)}, bf16[32,96,256]{2,1,0:T(8,128)(2,1)}, u32[]{:S(2)}) copy-start(bf16[32,96,256]{2,1,0:T(8,128)(2,1)} %param.25) | copy-start | bytes 4718596
  10.4 2.1 copy-start.4
  11.4 1.7 copy-start.16
  12.5 16.1 %copy-start.6 = (bf16[256,1024]{1,0:T(8,128)(2,1)S(1)}, bf16[256,1024]{1,0:T(8,128)(2,1)}, u32[]{:S(2)}) copy-start(bf16[256,1024]{1,0:T(8,128)(2,1)} %param.29) | copy-start | bytes 1572868
  80.9 2.7 copy-start.7
  80.9 2.9 copy-start.8
  80.9 23.4 %all-to-all-start = ((bf16[32,96,256]{2,0,1:T(8,128)(2,1)}), bf16[32,96,256]{2,0,1:T(8,128)(2,1)S(1)}, u32[]{:S(2)}, u32[]{:S(2)}) async-start(bf16[32,96,256]{2,0,1:T(8,128)(2,1)} %copy.139), calls=%async_computation | async-start | bytes 3145728 | tf_op jit(solution)/shard_map/all_to_all | solution.py:67
  83.4 108.1 %all-gather.2.cloned.1.call-start = ((), (), s32[]{:S(2)}) async-start(), calls=%async_computation.4 | async-start | bytes 1769472 | tf_op jit(solution)/shard_map/all_gather | solution.py:74
  164.3 3.7 %copy-start.3 = (bf16[8,256,12,32]{1,3,2,0:T(8,128)(2,1)S(1)}, bf16[8,256,12,32]{1,3,2,0:T(8,128)(2,1)}, u32[]{:S(2)}) copy-start(bf16[8,256,12,32]{1,3,2,0:T(8,128)(2,1)} %get-tuple-element.126) | copy-start | bytes 4718596
  168.0 3.1 %copy-start.15 = (bf16[256,64]{0,1:T(8,128)(2,1)S(1)}, bf16[256,64]{0,1:T(8,128)(2,1)}, u32[]{:S(2)}) copy-start(bf16[256,64]{0,1:T(8,128)(2,1)} %param.34) | copy-start | bytes 98308
  170.7 1.8 copy-start.9
  171.1 1.5 copy-start.17
  197.9 12.1 %copy-start.5 = (bf16[12,96,128]{2,1,0:T(8,128)(2,1)S(1)}, bf16[12,96,128]{2,1,0:T(8,128)(2,1)}, u32[]{:S(2)}) copy-start(bf16[12,96,128]{2,1,0:T(8,128)(2,1)} %param.26) | copy-start | bytes 884740
  210.0 4.4 %copy-start.13 = (bf16[128,4]{0,1:T(4,128)(2,1)S(1)}, bf16[128,4]{0,1:T(4,128)(2,1)}, u32[]{:S(2)}) copy-start(bf16[128,4]{0,1:T(4,128)(2,1)} %param.37) | copy-start | bytes 3076
  213.2 0.8 copy-start.2
  226.1 8.2 %copy-start.11 = (bf16[128,128]{1,0:T(8,128)(2,1)S(1)}, bf16[128,128]{1,0:T(8,128)(2,1)}, u32[]{:S(2)}) copy-start(bf16[128,128]{1,0:T(8,128)(2,1)} %param.38) | copy-start | bytes 98308
  234.3 4.6 %copy-start.10 = (bf16[128,512]{1,0:T(8,128)(2,1)S(1)}, bf16[128,512]{1,0:T(8,128)(2,1)}, u32[]{:S(2)}) copy-start(bf16[128,512]{1,0:T(8,128)(2,1)} %param.39) | copy-start | bytes 393220
  236.7 10.2 %all-to-all-start.2 = ((bf16[12,96,128]{2,0,1:T(8,128)(2,1)}), bf16[12,96,128]{2,0,1:T(8,128)(2,1)S(1)}, u32[]{:S(2)}, u32[]{:S(2)}) async-start(bf16[12,96,128]{2,0,1:T(8,128)(2,1)} %copy.155), calls=%async_computation.2 | async-start | bytes 786432 | tf_op jit(solution)/shard_map/all_to_all | solution.py:85
  246.9 41.2 %all-to-all-start.1 = ((bf16[256,12,256]{2,1,0:T(8,128)(2,1)}), bf16[256,12,256]{2,1,0:T(8,128)(2,1)}, u32[]{:S(2)}, u32[]{:S(2)}) async-start(bf16[256,12,256]{2,1,0:T(8,128)(2,1)} %copy.146), calls=%async_computation.1 | async-start | bytes 4194304 | tf_op jit(solution)/shard_map/all_to_all | solution.py:92
  251.1 1.1 copy-start.14
  281.2 5.7 %copy-start.12 = (bf16[128,128]{1,0:T(8,128)(2,1)S(1)}, bf16[128,128]{1,0:T(8,128)(2,1)}, u32[]{:S(2)}) copy-start(bf16[128,128]{1,0:T(8,128)(2,1)} %param.41) | copy-start | bytes 98308
  288.1 10.2 %all-to-all-start.3 = ((bf16[96,12,128]{2,1,0:T(8,128)(2,1)}), bf16[96,12,128]{2,1,0:T(8,128)(2,1)S(1)}, u32[]{:S(2)}, u32[]{:S(2)}) async-start(bf16[96,12,128]{2,1,0:T(8,128)(2,1)} %copy.163), calls=%async_computation.3 | async-start | bytes 786432 | tf_op jit(solution)/shard_map/all_to_all | solution.py:91
Sparse Core Ops, SparseCore 0:
  172.6 18.8 all-gather.1
where the time goes:
time: 308 us; the launch traced here: 306 us
  matrix products  123 us (40%)
  blocking collectives  54 us (18%)
  waiting for transfers between devices  47.8 us (16%)
  local copies, waits for them, and re-layouts  34.9 us (11%)
  other arithmetic  21.1 us (7%)
  between operations  14.6 us (5%)
  starting transfers between devices  10.1 us (3%)
    dot_general x24, matrix products, one_head(): jnp.einsum(forms[2], attn_prob, projected[:, :, 2], preferred_element_typ...  48.1 us
    sub x24, matrix products, one_head(): attn_prob = jax.nn.softmax(scores, axis=-1).astype(jnp.bfloat16)  39.7 us
    all_gather x1, blocking collectives, per_device(): end_bias = lax.all_gather(end_bias, group, axis=1, tiled=True)  28.6 us
    all_to_all x1, waiting for transfers between devices, per_device(): m_cols = lax.all_to_all(m_blk, group, 1, 0, tiled=True)  20.4 us
    all_gather x1, waiting for transfers between devices, per_device(): lax.all_gather(outer_proj[:, :, opm:] * col_w[:, :, None], group, axis=1,...  18.7 us
    convert_element_type x9, local copies, waits for them, and re-layouts, add_residual(): return (state.astype(jnp.float32) + update).astype(jnp.bfloat16)  15 us
    all_gather x1, blocking collectives, per_device(): row_bias = lax.all_gather(row_bias, group, axis=1, tiled=True)  14.1 us
    dot_general x24, matrix products, one_head(): jnp.einsum(forms[0], x_norm, head_in[0], preferred_element_type=jnp.float32)  14.1 us
  transfers between devices with their start and end apart: 5, of which 4 were waited for; matrix products, arithmetic and copies ran while one was open for 6% of the time, Pallas kernels for 0%

commit v1 on v0

v1 whole, which is shorter than its diff:
```python
import functools

import jax
import jax.numpy as jnp
from jax import lax
from jax.experimental import pallas as pl
from jax.experimental.pallas import tpu as pltpu
from jax.sharding import PartitionSpec as P

BF16 = jnp.bfloat16
F32 = jnp.float32
MESH = pl.DeviceIdType.MESH
NDEV = 8
SEQ, RES, CM, CZ = 256, 96, 256, 128
SLOC, RLOC = SEQ // NDEV, RES // NDEV
HM, HT, HD, OPM = 8, 4, 32, 32
LANES = 128
MASKED = -1e9
PADDED = -3e38
SCALE = HD ** -0.5

ROWB, MF0, MF1, MB, CG, STB, ZF, ENB, ZB = range(9)
NSTAGE = 9


def dot(a, b):
    return jnp.dot(a, b, preferred_element_type=F32)


def dot_t(a, b):
    return lax.dot_general(a, b, (((1,), (1,)), ((), ())), preferred_element_type=F32)


def iota(shape, dim):
    return lax.broadcasted_iota(jnp.int32, shape, dim)


def layer_norm(x):
    values = x.astype(F32)
    centred = values - jnp.mean(values, axis=-1, keepdims=True)
    variance = jnp.mean(centred * centred, axis=-1, keepdims=True)
    return (centred * lax.rsqrt(variance + 1e-5)).astype(BF16)


def add_residual(state, update):
    return (state.astype(F32) + update).astype(BF16)


def head_mask(head, channels):
    lane = iota((16, channels), 1)
    return jnp.where((lane >= head * HD) & (lane < (head + 1) * HD), 1.0, 0.0).astype(BF16)


def masked_head(x, head):
    rows, channels = x.shape
    return (x.reshape(rows // 16, 16, channels) * head_mask(head, channels)[None]).reshape(rows, channels)


def softmax_rows(logits):
    top = jnp.max(logits, axis=-1, keepdims=True)
    weights = jnp.exp(logits - top)
    return (weights * (1.0 / jnp.sum(weights, axis=-1, keepdims=True))).astype(BF16)


def attend_padded(q, k, v, g, bias_ref, keep, heads):
    out = None
    for pair in range(heads // 2):
        h0, h1 = 2 * pair, 2 * pair + 1
        kk = jnp.concatenate([masked_head(k, h0), masked_head(k, h1)], axis=0)
        scores = dot_t(q, kk)
        probs = []
        for u in range(2):
            logits = scores[:, u * LANES:(u + 1) * LANES] * SCALE + bias_ref[2 * pair + u]
            probs.append(softmax_rows(jnp.where(keep, logits, MASKED)))
        vv = jnp.concatenate([masked_head(v, h0), masked_head(v, h1)], axis=0)
        mixed = dot(jnp.concatenate(probs, axis=1), vv)
        out = mixed if out is None else out + mixed
    return (out * jax.nn.sigmoid(g.astype(F32))).astype(BF16)


def attend_column(q, k, v, g, keep):
    out = None
    for pair in range(HM // 2):
        probs, values = [], []
        for h in (2 * pair, 2 * pair + 1):
            logits = dot_t(q, masked_head(k, h)) * SCALE
            probs.append(softmax_rows(jnp.where(keep, logits, MASKED)))
            values.append(masked_head(v, h))
        mixed = dot(jnp.concatenate(probs, axis=1), jnp.concatenate(values, axis=0))
        out = mixed if out is None else out + mixed
    return (out * jax.nn.sigmoid(g.astype(F32))).astype(BF16)


def block_kernel(m_ref, z_ref, mask_ref, res_ref, w_row_in, w_row_bias, w_row_out, w_col_in, w_col_out,
                 w_opm_in, w_opm_out, w_start_in, w_start_bias, w_start_out, w_end_in, w_end_bias, w_end_out,
                 m_out, z_out,
                 perm, comp, hperm, keep_row, mask_t, norm, res_keep, wbt, bcol, bias,
                 rowb_recv, stb_recv, enb_recv, proj, gated, m1, msend, mcols, mback, colproj,
                 left, crecv, cbig, outer, w2, w2t, opm_in_t, ynorm, z1, zs, zr, z2, z3, zs2, zr2,
                 send_sem, recv_sem, local_sem):
    data = lax.axis_index('data')
    me = lax.axis_index('chip') * 4 + lax.axis_index('dap')

    def device(d):
        return (data, d // 4, lax.rem(d, 4))

    def peer(r):
        return lax.rem(me + r, NDEV)

    def source(r):
        return lax.rem(me + NDEV - r, NDEV)

    def start_all(stage, src_of, dst_of):
        for r in range(1, NDEV):
            d = peer(r)
            pltpu.make_async_remote_copy(src_ref=src_of(d), dst_ref=dst_of(me), send_sem=send_sem.at[stage, r],
                                         recv_sem=recv_sem.at[stage, r], device_id=device(d), device_id_type=MESH).start()

    def wait_recv(stage, src_of, dst_of):
        for r in range(1, NDEV):
            pltpu.make_async_remote_copy(src_ref=src_of(me), dst_ref=dst_of(source(r)), send_sem=send_sem.at[stage, r],
                                         recv_sem=recv_sem.at[stage, r], device_id=device(peer(r)),
                                         device_id_type=MESH).wait_recv()

    def wait_send(stage, src_of, dst_of):
        for r in range(1, NDEV):
            pltpu.make_async_remote_copy(src_ref=src_of(peer(r)), dst_ref=dst_of(me), send_sem=send_sem.at[stage, r],
                                         recv_sem=recv_sem.at[stage, r], device_id=device(peer(r)),
                                         device_id_type=MESH).wait_send()

    barrier = pltpu.get_barrier_semaphore()
    for r in range(1, NDEV):
        pl.semaphore_signal(barrier, inc=1, device_id=device(peer(r)), device_id_type=MESH)

    r0, c0 = iota((256, 256), 0), iota((256, 256), 1)
    perm[...] = jnp.where(((r0 >> 4) == (c0 & 15)) & ((r0 & 15) == (c0 >> 4)), 1.0, 0.0).astype(BF16)
    r1, c1 = iota((RES, LANES), 0), iota((RES, LANES), 1)
    comp[...] = jnp.where(((c1 & 15) < RLOC) & (r1 == (c1 >> 4) * RLOC + (c1 & 15)), 1.0, 0.0).astype(BF16)
    r2, c2 = iota((LANES, LANES), 0), iota((LANES, LANES), 1)
    hperm[...] = jnp.where(((r2 >> 4) == (c2 & 7)) & ((r2 & 15) == (c2 >> 3)), 1.0, 0.0).astype(BF16)
    bcol[...] = jnp.zeros_like(bcol)
    wbt[...] = jnp.zeros_like(wbt)
    for n, w in enumerate((w_row_bias, w_start_bias, w_end_bias)):
        wbt[n, 0:w.shape[1], :] = jnp.transpose(w[...].astype(F32))

    def send_bias(recv, which, heads, stage):
        weights = wbt[which].astype(BF16)

        @pl.loop(0, RLOC)
        def _(i):
            bcol[i, :, 0:RES] = dot_t(weights, ynorm[i])

        mine = dot(hperm[0:heads * 16, :], bcol[...].reshape(LANES, LANES).astype(BF16)).astype(BF16)
        rows = pl.ds(pl.multiple_of(me * 16, 16), 16)
        recv[:, rows, :] = mine.reshape(heads, 16, LANES)
        start_all(stage, lambda d: recv.at[:, rows, :], lambda s: recv.at[:, rows, :])

    def take_bias(recv, heads, stage):
        def rows_of(s):
            return recv.at[:, pl.ds(pl.multiple_of(s * 16, 16), 16), :]
        wait_recv(stage, rows_of, rows_of)
        lane = iota((RES, LANES), 1)
        for h in range(heads):
            bias[h] = jnp.where(lane < RES, dot(comp[...], recv[h]), PADDED)

    @pl.loop(0, RLOC)
    def _(i):
        ynorm[i] = layer_norm(z_ref[i])

    pl.semaphore_wait(barrier, NDEV - 1)
    send_bias(rowb_recv, 0, HM, ROWB)

    keep_row[...] = jnp.ones_like(keep_row)
    keep_row[:, 0:RES] = mask_ref[...]
    res_keep[...] = jnp.ones_like(res_keep)
    res_keep[0:1, 0:RES] = res_ref[...]
    eye = jnp.where(r2 == c2, 1.0, 0.0).astype(BF16)
    mask_bf = mask_ref[...].astype(F32).astype(BF16)
    mask_t[...] = jnp.zeros_like(mask_t)
    mask_t[0:RES, :] = dot_t(eye[0:RES, 0:RES], mask_bf)
    mt = mask_t[...].astype(BF16)
    norm[...] = dot_t(mt, mt)
    w_full = w_opm_out[...].reshape(OPM, OPM, CZ)
    for a in range(2):
        for c in range(2):
            blk = w_full[16 * a:16 * a + 16, 16 * c:16 * c + 16, :].reshape(256, CZ)
            w2[16 * c:16 * c + 16, 16 * a:16 * a + 16, :] = dot(perm[...], blk).astype(BF16).reshape(16, 16, CZ)
    w2t[...] = dot_t(eye, w2[...].reshape(OPM * OPM, CZ)).astype(BF16)
    opm_in_t[...] = jnp.transpose(w_opm_in[...].astype(F32)).astype(BF16)
    proj[:, RES:, :] = jnp.zeros((proj.shape[0], LANES - RES, 4 * CM), BF16)
    cbig[:, RES:, :] = jnp.zeros((OPM, LANES - RES, SEQ), BF16)
    z1[RLOC:, :, :] = jnp.zeros((16 - RLOC, RES, CZ), BF16)

    take_bias(rowb_recv, HM, ROWB)

    def m_src(half):
        return lambda d: msend.at[pl.ds(d * RLOC, RLOC), 16 * half:16 * half + 16, :]

    def m_dst(half):
        return lambda s: mcols.at[:, pl.ds(pl.multiple_of(s * SLOC + 16 * half, 16), 16), :]

    def local_copy(src, dst, n):
        return pltpu.make_async_copy(src, dst, local_sem.at[n])

    for half in range(2):
        @pl.loop(0, 4)
        def _(blk):
            s0 = half * 16 + blk * 4
            x = m_ref[pl.ds(s0, 4)].reshape(4 * RES, CM)
            proj[:, 0:RES, :] = dot(layer_norm(x), w_row_in[...]).astype(BF16).reshape(4, RES, 4 * CM)
            for u in range(4):
                keep = keep_row[pl.ds(me * SLOC + s0 + u, 1), :] != 0
                gated[u] = attend_padded(proj[u, 0:RES, 0:CM], proj[u, :, CM:2 * CM], proj[u, :, 2 * CM:3 * CM],
                                         proj[u, 0:RES, 3 * CM:4 * CM], bias, keep, HM)
            update = dot(gated[...].reshape(4 * RES, CM), w_row_out[...])
            m1[pl.ds(s0, 4)] = add_residual(x, update).reshape(4, RES, CM)

        for j in range(RES // 16):
            blk = m1[16 * half:16 * half + 16, 16 * j:16 * j + 16, :].reshape(256, CM)
            msend[16 * j:16 * j + 16, 16 * half:16 * half + 16, :] = dot(perm[...], blk).astype(BF16).reshape(16, 16, CM)
        start_all(MF0 + half, m_src(half), m_dst(half))
        local_copy(m_src(half)(me), m_dst(half)(me), half).start()

    for half in range(2):
        local_copy(m_src(half)(me), m_dst(half)(me), half).wait()
        wait_recv(MF0 + half, m_src(half), m_dst(half))

    @pl.loop(0, RLOC)
    def _(j):
        x = mcols[j]
        colproj[...] = dot(layer_norm(x), w_col_in[...]).astype(BF16)
        mask_row = mask_t[pl.ds(me * RLOC + j, 1), :]
        mixed = attend_column(colproj[:, 0:CM], colproj[:, CM:2 * CM], colproj[:, 2 * CM:3 * CM], colproj[:, 3 * CM:],
                              mask_row != 0.0)
        x = add_residual(x, dot(mixed, w_col_out[...]))
        mcols[j] = x
        start_all(MB, lambda d: mcols.at[j, pl.ds(pl.multiple_of(d * SLOC, SLOC), SLOC), :],
                  lambda s: mback.at[s * RLOC + j])
        both = dot_t(opm_in_t[...], layer_norm(x)).astype(BF16).astype(F32) * mask_row
        left[j] = both[0:OPM].astype(BF16)
        crecv[me * RLOC + j] = both[OPM:].astype(BF16)
        start_all(CG, lambda d: crecv.at[me * RLOC + j], lambda s: crecv.at[s * RLOC + j])

    mback[pl.ds(me * RLOC, RLOC)] = mcols[:, pl.ds(pl.multiple_of(me * SLOC, SLOC), SLOC), :]

    def c_rows(s):
        return crecv.at[pl.ds(s * RLOC, RLOC)]
    wait_recv(CG, c_rows, c_rows)
    for c in range(2):
        @pl.loop(0, RES // 16)
        def _(j):
            j0 = pl.multiple_of(j * 16, 16)
            blk = crecv[pl.ds(j0, 16), 16 * c:16 * c + 16, :].reshape(256, SEQ)
            cbig[16 * c:16 * c + 16, pl.ds(j0, 16), :] = dot(perm[...], blk).astype(BF16).reshape(16, 16, SEQ)

    @pl.loop(0, OPM // 2)
    def _(c):
        prod = dot_t(left[...].reshape(RLOC * OPM, SEQ), cbig[pl.ds(2 * c, 2)].reshape(256, SEQ)).astype(BF16)
        for u in range(2):
            outer[:, 2 * c + u] = prod[:, u * LANES:(u + 1) * LANES].reshape(RLOC, OPM, LANES)

    @pl.loop(0, RLOC)
    def _(i):
        update = dot(w2t[...], outer[i].reshape(OPM * OPM, LANES))
        update = update / (1e-3 + norm[pl.ds(me * RLOC + i, 1), :])
        z1[i] = add_residual(z_ref[i], jnp.transpose(update)[0:RES])

    def triangle(state, result, w_in, which, w_out, recv, stage):
        @pl.loop(0, RLOC)
        def _(i):
            ynorm[i] = layer_norm(state[i])
        send_bias(recv, which, HT, stage)
        take_bias(recv, HT, stage)
        keep = res_keep[0:1, :] != 0

        @pl.loop(0, RLOC // 4)
        def _(blk):
            i0 = blk * 4
            y = ynorm[pl.ds(i0, 4)].reshape(4 * RES, CZ)
            proj[:, 0:RES, 0:4 * CZ] = dot(y, w_in[...]).astype(BF16).reshape(4, RES, 4 * CZ)
            for u in range(4):
                gated[u, :, 0:CZ] = attend_padded(proj[u, 0:RES, 0:CZ], proj[u, :, CZ:2 * CZ], proj[u, :, 2 * CZ:3 * CZ],
                                                  proj[u, 0:RES, 3 * CZ:4 * CZ], bias, keep, HT)
            update = dot(gated[:, :, 0:CZ].reshape(4 * RES, CZ), w_out[...])
            x = state[pl.ds(i0, 4)].reshape(4 * RES, CZ)
            result[pl.ds(i0, 4)] = add_residual(x, update).reshape(4, RES, CZ)

    def z_src(buf):
        return lambda d: buf.at[pl.ds(d * RLOC, RLOC)]

    def z_dst(buf):
        return lambda s: buf.at[:, pl.ds(pl.multiple_of(s * 16, 16), 16), :]

    def exchange(state, send, recv, result, stage, n):
        for j in range(RES // 16):
            blk = state[:, 16 * j:16 * j + 16, :].reshape(256, CZ)
            send[16 * j:16 * j + 16] = dot(perm[...], blk).astype(BF16).reshape(16, 16, CZ)
        start_all(stage, z_src(send), z_dst(recv))
        own = local_copy(z_src(send)(me), z_dst(recv)(me), n)
        own.start()
        own.wait()
        wait_recv(stage, z_src(send), z_dst(recv))

        @pl.loop(0, RLOC)
        def _(i):
            result[i] = dot(comp[...], recv[i]).astype(BF16)

    triangle(z1, z1, w_start_in, 1, w_start_out, stb_recv, STB)
    exchange(z1, zs, zr, z2, ZF, 2)
    z3[RLOC:, :, :] = jnp.zeros((16 - RLOC, RES, CZ), BF16)
    triangle(z2, z3, w_end_in, 2, w_end_out, enb_recv, ENB)
    exchange(z3, zs2, zr2, z_out, ZB, 3)

    def mb_src(d):
        return mcols.at[:, pl.ds(pl.multiple_of(d * SLOC, SLOC), SLOC), :]

    def mb_dst(s):
        return mback.at[pl.ds(s * RLOC, RLOC)]
    wait_recv(MB, mb_src, mb_dst)
    for half in range(2):
        @pl.loop(0, RES // 16)
        def _(j):
            j0 = pl.multiple_of(j * 16, 16)
            blk = mback[pl.ds(j0, 16), 16 * half:16 * half + 16, :].reshape(256, CM)
            m_out[16 * half:16 * half + 16, pl.ds(j0, 16), :] = dot(perm[...], blk).astype(BF16).reshape(16, 16, CM)

    def b_rows(buf):
        return lambda s: buf.at[:, pl.ds(pl.multiple_of(me * 16, 16), 16), :]
    wait_send(ROWB, b_rows(rowb_recv), b_rows(rowb_recv))
    for half in range(2):
        wait_send(MF0 + half, m_src(half), m_dst(half))
    wait_send(MB, mb_src, mb_dst)
    wait_send(CG, lambda d: c_rows(me), c_rows)
    wait_send(STB, b_rows(stb_recv), b_rows(stb_recv))
    wait_send(ZF, z_src(zs), z_dst(zr))
    wait_send(ENB, b_rows(enb_recv), b_rows(enb_recv))
    wait_send(ZB, z_src(zs2), z_dst(zr2))


def solution(mesh):
    rows = P(('data', 'chip', 'dap'))
    in_specs = (rows, rows, P('data'), P('data')) + (P(),) * 13
    vmem = pl.BlockSpec(memory_space=pltpu.VMEM)

    def per_device(m_blk, z_blk, msa_mask, res_mask, *weights):
        scratch = [
            pltpu.VMEM((256, 256), BF16),
            pltpu.VMEM((RES, LANES), BF16),
            pltpu.VMEM((LANES, LANES), BF16),
            pltpu.VMEM((SEQ, LANES), jnp.int32),
            pltpu.VMEM((LANES, SEQ), F32),
            pltpu.VMEM((LANES, LANES), F32),
            pltpu.VMEM((8, LANES), jnp.int32),
            pltpu.VMEM((3, 8, CZ), F32),
            pltpu.VMEM((16, 8, LANES), F32),
            pltpu.VMEM((HM, RES, LANES), F32),
            pltpu.VMEM((HM, LANES, LANES), BF16),
            pltpu.VMEM((HT, LANES, LANES), BF16),
            pltpu.VMEM((HT, LANES, LANES), BF16),
            pltpu.VMEM((4, LANES, 4 * CM), BF16),
            pltpu.VMEM((4, RES, CM), BF16),
            pltpu.VMEM((SLOC, RES, CM), BF16),
            pltpu.VMEM((RES, SLOC, CM), BF16),
            pltpu.VMEM((RLOC, SEQ, CM), BF16),
            pltpu.VMEM((RES, SLOC, CM), BF16),
            pltpu.VMEM((SEQ, 4 * CM), BF16),
            pltpu.VMEM((RLOC, OPM, SEQ), BF16),
            pltpu.VMEM((RES, OPM, SEQ), BF16),
            pltpu.VMEM((OPM, LANES, SEQ), BF16),
            pltpu.VMEM((RLOC, OPM, OPM, LANES), BF16),
            pltpu.VMEM((OPM, OPM, CZ), BF16),
            pltpu.VMEM((CZ, OPM * OPM), BF16),
            pltpu.VMEM((2 * OPM, CM), BF16),
            pltpu.VMEM((RLOC, RES, CZ), BF16),
            pltpu.VMEM((16, RES, CZ), BF16),
            pltpu.VMEM((RES, 16, CZ), BF16),
            pltpu.VMEM((RLOC, LANES, CZ), BF16),
            pltpu.VMEM((RLOC, RES, CZ), BF16),
            pltpu.VMEM((16, RES, CZ), BF16),
            pltpu.VMEM((RES, 16, CZ), BF16),
            pltpu.VMEM((RLOC, LANES, CZ), BF16),
            pltpu.SemaphoreType.DMA((NSTAGE, NDEV)),
            pltpu.SemaphoreType.DMA((NSTAGE, NDEV)),
            pltpu.SemaphoreType.DMA((4,)),
        ]
        return pl.pallas_call(
            block_kernel,
            name='evoformer_block',
            out_shape=(jax.ShapeDtypeStruct(m_blk.shape, BF16), jax.ShapeDtypeStruct(z_blk.shape, BF16)),
            in_specs=[vmem] * 17,
            out_specs=(vmem, vmem),
            scratch_shapes=scratch,
            compiler_params=pltpu.CompilerParams(collective_id=0, has_side_effects=True,
                                                 vmem_limit_bytes=56 * 1024 * 1024),
        )(m_blk, z_blk, msa_mask, res_mask.reshape(1, RES), *weights)

    return jax.shard_map(per_device, mesh=mesh, in_specs=in_specs, out_specs=(rows, rows), check_vma=False)
```

time: 308 us -> 153 us (0.50)
  Pallas kernels: 0 us -> 141 us
  matrix products: 123 us -> 0 us
  blocking collectives: 54 us -> 0 us
  waiting for transfers between devices: 47.8 us -> 0 us
  local copies, waits for them, and re-layouts: 34.9 us -> 10.7 us
  other arithmetic: 21.1 us -> 0 us
  between operations: 14.6 us -> 0.65 us
  starting transfers between devices: 10.1 us -> 0 us
    pallas_call x0 -> x1, Pallas kernels: none -> 141 us  [per_device(): pl.pallas_call(block_kernel, name='evoformer_block', out_shape=(jax.Shape...]
    dot_general x67 -> x0, matrix products: 83.4 us -> none  [the longest x24 48.1 us: one_head(): jnp.einsum(forms[2], attn_prob, projected[:, :, 2], preferred_element_typ...]
    all_gather x3 -> x0, blocking collectives: 54 us -> none  [the longest x1 28.6 us: per_device(): end_bias = lax.all_gather(end_bias, group, axis=1, tiled=True)]
    sub x24 -> x0, matrix products: 39.7 us -> none  [one_head(): attn_prob = jax.nn.softmax(scores, axis=-1).astype(jnp.bfloat16)]
    all_to_all x4 -> x0, waiting for transfers between devices: 29.1 us -> none  [the longest x1 20.4 us: per_device(): m_cols = lax.all_to_all(m_blk, group, 1, 0, tiled=True)]
    convert_element_type x10 -> x0, local copies, waits for them, and re-layouts: 27.1 us -> none  [the longest x9 15 us: add_residual(): return (state.astype(jnp.float32) + update).astype(jnp.bfloat16)]
    all_gather x1 -> x0, waiting for transfers between devices: 18.7 us -> none  [per_device(): lax.all_gather(outer_proj[:, :, opm:] * col_w[:, :, None], group, axis=1,...]
    all_to_all x4 -> x0, starting transfers between devices: 9.89 us -> none  [the longest x1 3.07 us: per_device(): m_out = lax.all_to_all(m_cols, group, 0, 1, tiled=True)]
  transfers between devices with their start and end apart: 5 -> 0, of which waited for: 4 -> 0; matrix products, arithmetic and copies ran while one was open for 6% -> 0% of each run, Pallas kernels for 0% -> 0%
where the time goes in v1:
time: 153 us; the launch traced here: 152 us
  Pallas kernels  141 us (92%)
  local copies, waits for them, and re-layouts  10.7 us (7%)
    pallas_call x1, Pallas kernels, per_device(): pl.pallas_call(block_kernel, name='evoformer_block', out_shape=(jax.Shape...  141 us
    unnamed x9, local copies, waits for them, and re-layouts  10.7 us

profile of v1, /device:TPU:0, one launch (start us, length us, event | category | flops | bytes accessed | tf_op | source)
XLA Modules:
  0.0 152.3 jit_solution(12524985032859886541)
XLA Ops:
  0.6 1.4 copy.20.w_row_bias
  2.0 1.4 copy.22.w_start_bias
  3.4 1.4 copy.23.w_end_bias
  4.8 1.5 copy.21.w_opm_in
  6.3 1.6 %copy.19.mask_ref = s32[256,96]{1,0:T(8,128)} copy(s32[256,96]{0,1:T(8,128)} %param.19) | data formatting | bytes 196608 | tf_op args[2]
  7.9 140.9 %evoformer_block.1 = (bf16[32,96,256]{2,1,0:T(8,128)(2,1)}, bf16[12,96,128]{2,1,0:T(8,128)(2,1)}) custom-call(bf16[32,96,256]{2,1,0:T(8,128)(2,1)} %m_ref.1, bf16[12,96,128]{2,1,0:T(8,128)(2,1)} %z_ref.1, s32[256,96]{1,0:T(8,128)} %copy.19.mask_ref, s32[1,96]{1,0:T(1,128)} %bitcast.1, bf16[256,1024]{1,0:T(8,128)(2,1)} %w_row_in.1, ...), custom_call_target="tpu_custom_call" | custom-call | tf_op jit(solution)/shard_map/evoformer_block/pallas_call | solution.py:386
  148.9 0.0 copy-start
  148.9 2.7 %copy.26 = bf16[32,96,256]{2,1,0:T(8,128)(2,1)} copy(bf16[32,96,256]{2,1,0:T(8,128)(2,1)} %get-tuple-element.4) | data formatting | bytes 3145728
  151.6 0.0 copy-done
  151.6 0.7 copy.27
Async XLA Ops:
  148.9 2.7 %copy-start = (bf16[12,96,128]{2,1,0:T(8,128)(2,1)S(1)}, bf16[12,96,128]{2,1,0:T(8,128)(2,1)}, u32[]{:S(2)}) copy-start(bf16[12,96,128]{2,1,0:T(8,128)(2,1)} %get-tuple-element.5) | copy-start | bytes 884740

commit v2 on v1

v2 whole, which is shorter than its diff:
```python
import functools

import jax
import jax.numpy as jnp
from jax import lax
from jax.experimental import pallas as pl
from jax.experimental.pallas import tpu as pltpu
from jax.sharding import PartitionSpec as P

BF16 = jnp.bfloat16
F32 = jnp.float32
MESH = pl.DeviceIdType.MESH
NDEV = 8
SEQ, RES, CM, CZ = 256, 96, 256, 128
SLOC, RLOC = SEQ // NDEV, RES // NDEV
HM, HT, HD, OPM = 8, 4, 32, 32
LANES = 128
MASKED = -1e9
PADDED = -3e38
SCALE = HD ** -0.5

ROWB, MF, MB, STB, ZF, ENB, ZB = 0, 1, 5, 6, 7, 8, 9
NSTAGE = 10
CHUNK = 8
NCHUNK = SLOC // CHUNK
CROWS = NDEV * CHUNK
LAG = 2
MB_EARLY = 6


def dot(a, b):
    return jnp.dot(a, b, preferred_element_type=F32)


def dot_t(a, b):
    return lax.dot_general(a, b, (((1,), (1,)), ((), ())), preferred_element_type=F32)


def iota(shape, dim):
    return lax.broadcasted_iota(jnp.int32, shape, dim)


def layer_norm(x):
    values = x.astype(F32)
    centred = values - jnp.mean(values, axis=-1, keepdims=True)
    variance = jnp.mean(centred * centred, axis=-1, keepdims=True)
    return (centred * lax.rsqrt(variance + 1e-5)).astype(BF16)


def add_residual(state, update):
    return (state.astype(F32) + update).astype(BF16)


def head_masks():
    lane = iota((16, LANES), 1)
    return [jnp.where((lane >= h * HD) & (lane < (h + 1) * HD), 1.0, 0.0).astype(BF16) for h in range(LANES // HD)]


def only_head(x, mask):
    return (x.reshape(x.shape[0] // 16, 16, LANES) * mask[None]).reshape(x.shape)


def softmax_rows(logits):
    top = jnp.max(logits, axis=-1, keepdims=True)
    weights = jnp.exp(logits - top)
    return (weights * (1.0 / jnp.sum(weights, axis=-1, keepdims=True))).astype(BF16)


def gate(tiles, g):
    mixed = tiles[0] if len(tiles) == 1 else jnp.concatenate(tiles, axis=1)
    return (mixed * jax.nn.sigmoid(g.astype(F32))).astype(BF16)


def attend_padded(q, k, v, g, bias_ref, keep, heads):
    masks = head_masks()
    tiles = []
    for t in range(heads // 4):
        lanes = slice(t * LANES, (t + 1) * LANES)
        probs = []
        for pair in range(2):
            kk = jnp.concatenate([only_head(k[:, lanes], masks[2 * pair + u]) for u in range(2)], axis=0)
            scores = dot_t(q[:, lanes], kk)
            for u in range(2):
                logits = scores[:, u * LANES:(u + 1) * LANES] * SCALE + bias_ref[4 * t + 2 * pair + u]
                probs.append(softmax_rows(jnp.where(keep, logits, MASKED)))
        vv = jnp.concatenate([only_head(v[:, lanes], mask) for mask in masks], axis=0)
        tiles.append(dot(jnp.concatenate(probs, axis=1), vv))
    return gate(tiles, g)


def attend_column(q, k, v, g, keep):
    masks = head_masks()
    tiles = []
    for t in range(HM // 4):
        lanes = slice(t * LANES, (t + 1) * LANES)
        probs = []
        for mask in masks:
            logits = dot_t(q[:, lanes], only_head(k[:, lanes], mask)) * SCALE
            probs.append(softmax_rows(jnp.where(keep, logits, MASKED)))
        vv = jnp.concatenate([only_head(v[:, lanes], mask) for mask in masks], axis=0)
        tiles.append(dot(jnp.concatenate(probs, axis=1), vv))
    return gate(tiles, g)


def block_kernel(m_ref, z_ref, mask_ref, res_ref, w_row_in, w_row_bias, w_row_out, w_col_in, w_col_out,
                 w_opm_in, w_opm_out, w_start_in, w_start_bias, w_start_out, w_end_in, w_end_bias, w_end_out,
                 m_out, z_out,
                 perm, perm_out, perm_in, comp, hperm, keep_row, mask_t, norm, res_keep, wbt, bcol, bias,
                 rowb_recv, stb_recv, enb_recv, proj, gated, projt, m1, msend, mcols, mback, colproj,
                 left, crecv, cbig, outer, w2, w2t, ynorm, z1, zs, zr, z2, z3, zs2, zr2,
                 send_sem, recv_sem, local_sem, c_send, c_recv, c_pair):
    data = lax.axis_index('data')
    me = lax.axis_index('chip') * 4 + lax.axis_index('dap')
    core, chip_x, chip_y = lax.rem(me, 2), lax.rem(me // 2, 2), me // 4
    partner = me + 1 - 2 * core
    to_x, to_y = 2 - 4 * chip_x, 4 - 8 * chip_y
    twins = (me + to_x + to_y, me + to_x, me + to_y)

    def device(d):
        return (data, d // 4, lax.rem(d, 4))

    def peer(r):
        return lax.rem(me + r, NDEV)

    def source(r):
        return lax.rem(me + NDEV - r, NDEV)

    def remote(src, dst, send, recv, d):
        return pltpu.make_async_remote_copy(src_ref=src, dst_ref=dst, send_sem=send, recv_sem=recv,
                                            device_id=device(d), device_id_type=MESH)

    def start_all(stage, src_of, dst_of):
        for r in range(1, NDEV):
            d = peer(r)
            remote(src_of(d), dst_of(me), send_sem.at[stage, r], recv_sem.at[stage, r], d).start()

    def wait_recv(stage, dst_of):
        for r in range(1, NDEV):
            dst = dst_of(source(r))
            remote(dst, dst, send_sem.at[stage, r], recv_sem.at[stage, r], peer(r)).wait_recv()

    def wait_send(stage, src_of):
        for r in range(1, NDEV):
            src = src_of(peer(r))
            remote(src, src, send_sem.at[stage, r], recv_sem.at[stage, r], peer(r)).wait_send()

    barrier = pltpu.get_barrier_semaphore()
    for r in range(1, NDEV):
        pl.semaphore_signal(barrier, inc=1, device_id=device(peer(r)), device_id_type=MESH)

    r0, c0 = iota((256, 256), 0), iota((256, 256), 1)
    perm[...] = jnp.where(((r0 >> 4) == (c0 & 15)) & ((r0 & 15) == (c0 >> 4)), 1.0, 0.0).astype(BF16)
    perm_out[...] = jnp.where(((r0 >> 3) == (c0 & 31)) & ((r0 & 7) == (c0 >> 5)), 1.0, 0.0).astype(BF16)
    perm_in[...] = jnp.where(((r0 >> 5) == (c0 & 7)) & ((r0 & 31) == (c0 >> 3)), 1.0, 0.0).astype(BF16)
    r1, c1 = iota((RES, LANES), 0), iota((RES, LANES), 1)
    comp[...] = jnp.where(((c1 & 15) < RLOC) & (r1 == (c1 >> 4) * RLOC + (c1 & 15)), 1.0, 0.0).astype(BF16)
    r2, c2 = iota((LANES, LANES), 0), iota((LANES, LANES), 1)
    hperm[...] = jnp.where(((r2 >> 4) == (c2 & 7)) & ((r2 & 15) == (c2 >> 3)), 1.0, 0.0).astype(BF16)
    bcol[...] = jnp.zeros_like(bcol)
    wbt[...] = jnp.zeros_like(wbt)
    for n, w in enumerate((w_row_bias, w_start_bias, w_end_bias)):
        wbt[n, 0:w.shape[0], :] = w[...].astype(F32)

    def send_bias(recv, which, heads, stage):
        weights = wbt[which].astype(BF16)

        @pl.loop(0, RLOC)
        def _(i):
            bcol[i, :, 0:RES] = dot_t(weights, ynorm[i])

        mine = dot(hperm[0:heads * 16, :], bcol[...].reshape(LANES, LANES).astype(BF16)).astype(BF16)
        rows = pl.ds(pl.multiple_of(me * 16, 16), 16)
        recv[:, rows, :] = mine.reshape(heads, 16, LANES)
        start_all(stage, lambda d: recv.at[:, rows, :], lambda s: recv.at[:, rows, :])

    def bias_rows(recv):
        return lambda s: recv.at[:, pl.ds(pl.multiple_of(s * 16, 16), 16), :]

    def take_bias(recv, heads, stage):
        wait_recv(stage, bias_rows(recv))
        lane = iota((RES, LANES), 1)
        for h in range(heads):
            bias[h] = jnp.where(lane < RES, dot(comp[...], recv[h]), PADDED)

    @pl.loop(0, RLOC)
    def _(i):
        ynorm[i] = layer_norm(z_ref[i])

    pl.semaphore_wait(barrier, NDEV - 1)
    send_bias(rowb_recv, 0, HM, ROWB)

    res_keep[...] = jnp.ones_like(res_keep)
    res_keep[0:1, 0:RES] = res_ref[...]
    eye = jnp.where(r2 == c2, 1.0, 0.0).astype(BF16)
    eye256 = jnp.where(r0 == c0, 1.0, 0.0).astype(BF16)
    seq_order = jnp.where(r0 == ((c0 >> 3) & 7) * SLOC + (c0 >> 6) * CHUNK + (c0 & 7), 1.0, 0.0).astype(BF16)
    mt = mask_ref[...].astype(F32).astype(BF16)
    keep_row[...] = jnp.ones_like(keep_row)
    keep_row[:, 0:RES] = dot_t(eye256, mt)
    mask_t[...] = dot(mt, seq_order)
    norm[...] = jnp.zeros_like(norm)
    norm[0:RES, 0:RES] = dot_t(mt, mt)
    w_full = w_opm_out[...].reshape(OPM, OPM, CZ)
    for a in range(2):
        for c in range(2):
            blk = w_full[16 * a:16 * a + 16, 16 * c:16 * c + 16, :].reshape(256, CZ)
            w2[16 * c:16 * c + 16, 16 * a:16 * a + 16, :] = dot(perm[...], blk).astype(BF16).reshape(16, 16, CZ)
    w2t[...] = dot_t(eye, w2[...].reshape(OPM * OPM, CZ)).astype(BF16)
    proj[:, RES:, :] = jnp.zeros((proj.shape[0], LANES - RES, 4 * CM), BF16)
    projt[:, RES:, :] = jnp.zeros((RLOC, LANES - RES, 4 * CZ), BF16)
    cbig[:, RES:, :] = jnp.zeros((OPM, LANES - RES, SEQ), BF16)
    z1[RLOC:, :, :] = jnp.zeros((16 - RLOC, RES, CZ), BF16)
    z3[RLOC:, :, :] = jnp.zeros((16 - RLOC, RES, CZ), BF16)

    take_bias(rowb_recv, HM, ROWB)

    def m_src(q):
        return lambda d: msend.at[q, pl.ds(d * RLOC, RLOC)]

    def m_dst(q):
        return lambda s: mcols.at[q, :, pl.ds(pl.multiple_of(s * CHUNK, CHUNK), CHUNK), :]

    def local_copy(src, dst, n):
        return pltpu.make_async_copy(src, dst, local_sem.at[n])

    def row_chunk(q):
        @pl.loop(0, CHUNK // 4)
        def _(blk):
            s0 = q * CHUNK + blk * 4
            x = m_ref[pl.ds(s0, 4)].reshape(4 * RES, CM)
            proj[:, 0:RES, :] = dot(layer_norm(x), w_row_in[...]).astype(BF16).reshape(4, RES, 4 * CM)
            for u in range(4):
                keep = keep_row[pl.ds(me * SLOC + s0 + u, 1), :] != 0.0
                gated[u] = attend_padded(proj[u, 0:RES, 0:CM], proj[u, :, CM:2 * CM], proj[u, :, 2 * CM:3 * CM],
                                         proj[u, 0:RES, 3 * CM:4 * CM], bias, keep, HM)
            update = dot(gated[...].reshape(4 * RES, CM), w_row_out[...])
            m1[pl.ds(s0, 4)] = add_residual(x, update).reshape(4, RES, CM)

        for j in range(RES // 32):
            blk = m1[CHUNK * q:CHUNK * q + CHUNK, 32 * j:32 * j + 32, :].reshape(256, CM)
            msend[q, 32 * j:32 * j + 32] = dot(perm_out[...], blk).reshape(32, CHUNK, CM).astype(BF16)
        start_all(MF + q, m_src(q), m_dst(q))
        local_copy(m_src(q)(me), m_dst(q)(me), q).start()

    def column_projection(q):
        local_copy(m_src(q)(me), m_dst(q)(me), q).wait()
        wait_recv(MF + q, m_dst(q))

        @pl.loop(0, RLOC // 4)
        def _(blk):
            x = mcols[q, pl.ds(blk * 4, 4)].reshape(4 * CROWS, CM)
            y = dot(layer_norm(x), w_col_in[...]).astype(BF16).reshape(4, CROWS, 4 * CM)
            colproj[pl.ds(blk * 4, 4), CROWS * q:CROWS * q + CROWS, :] = y

    row_chunk(0)
    row_chunk(1)
    row_chunk(2)
    column_projection(0)
    row_chunk(3)
    column_projection(1)
    column_projection(2)
    column_projection(3)

    def mb_start(j):
        start_all(MB, lambda d: mcols.at[:, j, pl.ds(pl.multiple_of(d * CHUNK, CHUNK), CHUNK), :],
                  lambda s: mback.at[:, pl.ds(pl.multiple_of((s * RLOC + j) * CHUNK, CHUNK), CHUNK), :])

    def relay(j):
        for t, twin in enumerate(twins):
            row = crecv.at[twin * RLOC + j]
            remote(row, row, c_send.at[t], c_recv.at[t, j], twin).wait_recv()
            remote(row, row, c_send.at[3 + t], c_pair.at[t], partner).start()

    @pl.loop(0, RLOC)
    def _(j):
        x = mcols[:, j].reshape(SEQ, CM)
        mask_row = mask_t[pl.ds(me * RLOC + j, 1), :]
        mixed = attend_column(colproj[j, :, 0:CM], colproj[j, :, CM:2 * CM], colproj[j, :, 2 * CM:3 * CM],
                              colproj[j, :, 3 * CM:], mask_row != 0.0)
        x = add_residual(x, dot(mixed, w_col_out[...]))
        both = dot_t(w_opm_in[...], layer_norm(x)).astype(BF16).astype(F32) * mask_row
        left[j] = both[0:OPM].astype(BF16)
        crecv[me * RLOC + j] = both[OPM:].astype(BF16)
        row = crecv.at[me * RLOC + j]
        for t, twin in enumerate(twins):
            remote(row, row, c_send.at[t], c_recv.at[t, j], twin).start()
        remote(row, row, c_send.at[6], c_pair.at[3], partner).start()
        mcols[:, j] = x.reshape(NCHUNK, CROWS, CM)

        @pl.when(j >= LAG)
        def _():
            relay(j - LAG)

        @pl.when(j < MB_EARLY)
        def _():
            mb_start(j)

    for j in range(RLOC - LAG, RLOC):
        relay(j)
    for q in range(NCHUNK):
        mine = mcols[q, :, pl.ds(pl.multiple_of(me * CHUNK, CHUNK), CHUNK), :]
        mback[q, pl.ds(pl.multiple_of(me * (RLOC * CHUNK), 32), RLOC * CHUNK), :] = mine.reshape(RLOC * CHUNK, CM)

    def c_rows(s):
        return crecv.at[pl.ds(s * RLOC, RLOC)]

    for t, first in enumerate(twins + (me,)):
        rows = c_rows(first + 1 - 2 * core)
        remote(rows, rows, c_send.at[3 + t], c_pair.at[t], partner).wait_recv()
    for j in range(MB_EARLY, MB_EARLY + 3):
        mb_start(j)
    for c in range(2):
        @pl.loop(0, RES // 16)
        def _(j):
            j0 = pl.multiple_of(j * 16, 16)
            blk = crecv[pl.ds(j0, 16), 16 * c:16 * c + 16, :].reshape(256, SEQ)
            cbig[16 * c:16 * c + 16, pl.ds(j0, 16), :] = dot(perm[...], blk).astype(BF16).reshape(16, 16, SEQ)

    @pl.loop(0, OPM // 2)
    def _(c):
        prod = dot_t(left[...].reshape(RLOC * OPM, SEQ), cbig[pl.ds(2 * c, 2)].reshape(256, SEQ)).astype(BF16)
        for u in range(2):
            outer[:, 2 * c + u] = prod[:, u * LANES:(u + 1) * LANES].reshape(RLOC, OPM, LANES)

    @pl.loop(0, RLOC)
    def _(i):
        update = dot(w2t[...], outer[i].reshape(OPM * OPM, LANES))
        update = update / (1e-3 + norm[pl.ds(me * RLOC + i, 1), :])
        z1[i] = add_residual(z_ref[i], jnp.transpose(update)[0:RES])

    def triangle(state, result, w_in, which, w_out, recv, stage, late):
        @pl.loop(0, RLOC)
        def _(i):
            ynorm[i] = layer_norm(state[i])
        send_bias(recv, which, HT, stage)

        @pl.loop(0, RLOC // 4)
        def _(blk):
            y = ynorm[pl.ds(blk * 4, 4)].reshape(4 * RES, CZ)
            projt[pl.ds(blk * 4, 4), 0:RES, :] = dot(y, w_in[...]).astype(BF16).reshape(4, RES, 4 * CZ)
        take_bias(recv, HT, stage)
        for j in late:
            mb_start(j)
        keep = res_keep[0:1, :] != 0

        @pl.loop(0, RLOC // 4)
        def _(blk):
            i0 = blk * 4
            for u in range(4):
                i = i0 + u
                gated[u, :, 0:CZ] = attend_padded(projt[i, 0:RES, 0:CZ], projt[i, :, CZ:2 * CZ],
                                                  projt[i, :, 2 * CZ:3 * CZ], projt[i, 0:RES, 3 * CZ:4 * CZ],
                                                  bias, keep, HT)
            update = dot(gated[:, :, 0:CZ].reshape(4 * RES, CZ), w_out[...])
            x = state[pl.ds(i0, 4)].reshape(4 * RES, CZ)
            result[pl.ds(i0, 4)] = add_residual(x, update).reshape(4, RES, CZ)

    def z_src(buf):
        return lambda d: buf.at[pl.ds(d * RLOC, RLOC)]

    def z_dst(buf):
        return lambda s: buf.at[:, pl.ds(pl.multiple_of(s * 16, 16), 16), :]

    def exchange(state, send, recv, result, stage, n):
        for j in range(RES // 16):
            blk = state[:, 16 * j:16 * j + 16, :].reshape(256, CZ)
            send[16 * j:16 * j + 16] = dot(perm[...], blk).astype(BF16).reshape(16, 16, CZ)
        start_all(stage, z_src(send), z_dst(recv))
        own = local_copy(z_src(send)(me), z_dst(recv)(me), n)
        own.start()
        own.wait()
        wait_recv(stage, z_dst(recv))

        @pl.loop(0, RLOC)
        def _(i):
            result[i] = dot(comp[...], recv[i]).astype(BF16)

    triangle(z1, z1, w_start_in, 1, w_start_out, stb_recv, STB, (MB_EARLY + 3, MB_EARLY + 4))
    exchange(z1, zs, zr, z2, ZF, NCHUNK)
    triangle(z2, z3, w_end_in, 2, w_end_out, enb_recv, ENB, (MB_EARLY + 5,))
    exchange(z3, zs2, zr2, z_out, ZB, NCHUNK + 1)

    def mb_dst(s):
        return mback.at[:, pl.ds(pl.multiple_of(s * (RLOC * CHUNK), 32), RLOC * CHUNK), :]
    wait_recv(MB, mb_dst)
    for q in range(NCHUNK):
        @pl.loop(0, RES // 32)
        def _(j):
            blk = mback[q, pl.ds(pl.multiple_of(j * 256, 256), 256), :]
            rows = dot(perm_in[...], blk).astype(BF16).reshape(CHUNK, 32, CM)
            m_out[CHUNK * q:CHUNK * q + CHUNK, pl.ds(pl.multiple_of(j * 32, 32), 32), :] = rows

    wait_send(ROWB, lambda d: bias_rows(rowb_recv)(me))
    for q in range(NCHUNK):
        wait_send(MF + q, m_src(q))
    wait_send(MB, lambda d: mcols.at[:, :, pl.ds(pl.multiple_of(d * CHUNK, CHUNK), CHUNK), :])
    for t in range(7):
        rows = c_rows(me if t in (0, 1, 2, 6) else twins[t - 3])
        remote(rows, rows, c_send.at[t], c_pair.at[0], partner).wait_send()
    wait_send(STB, lambda d: bias_rows(stb_recv)(me))
    wait_send(ZF, z_src(zs))
    wait_send(ENB, lambda d: bias_rows(enb_recv)(me))
    wait_send(ZB, z_src(zs2))


def solution(mesh):
    rows = P(('data', 'chip', 'dap'))
    in_specs = (rows, rows, P('data'), P('data')) + (P(),) * 13
    vmem = pl.BlockSpec(memory_space=pltpu.VMEM)

    def per_device(m_blk, z_blk, msa_mask, res_mask, w_row_in, w_row_bias, w_row_out, w_col_in, w_col_out,
                   w_opm_in, w_opm_out, w_start_in, w_start_bias, w_start_out, w_end_in, w_end_bias, w_end_out):
        scratch = [
            pltpu.VMEM((256, 256), BF16),
            pltpu.VMEM((256, 256), BF16),
            pltpu.VMEM((256, 256), BF16),
            pltpu.VMEM((RES, LANES), BF16),
            pltpu.VMEM((LANES, LANES), BF16),
            pltpu.VMEM((SEQ, LANES), F32),
            pltpu.VMEM((RES, SEQ), F32),
            pltpu.VMEM((LANES, LANES), F32),
            pltpu.VMEM((8, LANES), jnp.int32),
            pltpu.VMEM((3, 8, CZ), F32),
            pltpu.VMEM((16, 8, LANES), F32),
            pltpu.VMEM((HM, RES, LANES), F32),
            pltpu.VMEM((HM, LANES, LANES), BF16),
            pltpu.VMEM((HT, LANES, LANES), BF16),
            pltpu.VMEM((HT, LANES, LANES), BF16),
            pltpu.VMEM((4, LANES, 4 * CM), BF16),
            pltpu.VMEM((4, RES, CM), BF16),
            pltpu.VMEM((RLOC, LANES, 4 * CZ), BF16),
            pltpu.VMEM((SLOC, RES, CM), BF16),
            pltpu.VMEM((NCHUNK, RES, CHUNK, CM), BF16),
            pltpu.VMEM((NCHUNK, RLOC, CROWS, CM), BF16),
            pltpu.VMEM((NCHUNK, RES * CHUNK, CM), BF16),
            pltpu.VMEM((RLOC, SEQ, 4 * CM), BF16),
            pltpu.VMEM((RLOC, OPM, SEQ), BF16),
            pltpu.VMEM((RES, OPM, SEQ), BF16),
            pltpu.VMEM((OPM, LANES, SEQ), BF16),
            pltpu.VMEM((RLOC, OPM, OPM, LANES), BF16),
            pltpu.VMEM((OPM, OPM, CZ), BF16),
            pltpu.VMEM((CZ, OPM * OPM), BF16),
            pltpu.VMEM((RLOC, RES, CZ), BF16),
            pltpu.VMEM((16, RES, CZ), BF16),
            pltpu.VMEM((RES, 16, CZ), BF16),
            pltpu.VMEM((RLOC, LANES, CZ), BF16),
            pltpu.VMEM((RLOC, RES, CZ), BF16),
            pltpu.VMEM((16, RES, CZ), BF16),
            pltpu.VMEM((RES, 16, CZ), BF16),
            pltpu.VMEM((RLOC, LANES, CZ), BF16),
            pltpu.SemaphoreType.DMA((NSTAGE, NDEV)),
            pltpu.SemaphoreType.DMA((NSTAGE, NDEV)),
            pltpu.SemaphoreType.DMA((NCHUNK + 2,)),
            pltpu.SemaphoreType.DMA((7,)),
            pltpu.SemaphoreType.DMA((3, RLOC)),
            pltpu.SemaphoreType.DMA((4,)),
        ]
        return pl.pallas_call(
            block_kernel,
            name='evoformer_block',
            out_shape=(jax.ShapeDtypeStruct(m_blk.shape, BF16), jax.ShapeDtypeStruct(z_blk.shape, BF16)),
            in_specs=[vmem] * 17,
            out_specs=(vmem, vmem),
            scratch_shapes=scratch,
            compiler_params=pltpu.CompilerParams(collective_id=0, has_side_effects=True,
                                                 vmem_limit_bytes=56 * 1024 * 1024),
        )(m_blk, z_blk, msa_mask.T, res_mask.reshape(1, RES), w_row_in, w_row_bias.T, w_row_out, w_col_in, w_col_out,
          w_opm_in.T, w_opm_out, w_start_in, w_start_bias.T, w_start_out, w_end_in, w_end_bias.T, w_end_out)

    return jax.shard_map(per_device, mesh=mesh, in_specs=in_specs, out_specs=(rows, rows), check_vma=False)
```

time: 153 us -> 140 us (0.915)
  local copies, waits for them, and re-layouts: 10.7 us -> 3.41 us
  Pallas kernels: 141 us -> 136 us
    unnamed x9 -> x4, local copies, waits for them, and re-layouts: 10.7 us -> 3.41 us
    pallas_call x1, Pallas kernels: 141 us -> 136 us  [per_device(): pl.pallas_call(block_kernel, name='evoformer_block', out_shape=(jax.Shape...]
where the time goes in v2:
time: 140 us
  Pallas kernels  136 us (97%)
  local copies, waits for them, and re-layouts  3.41 us (2%)
    pallas_call x1, Pallas kernels, per_device(): pl.pallas_call(block_kernel, name='evoformer_block', out_shape=(jax.Shape...  136 us
    unnamed x4, local copies, waits for them, and re-layouts  3.41 us

profile of v2, /device:TPU:0, one launch (start us, length us, event | category | flops | bytes accessed | tf_op | source)
XLA Modules:
  0.0 140.1 jit_solution(1249858152285689555)
XLA Ops:
  0.6 136.0 %evoformer_block.1 = (bf16[32,96,256]{2,1,0:T(8,128)(2,1)}, bf16[12,96,128]{2,1,0:T(8,128)(2,1)}) custom-call(bf16[32,96,256]{2,1,0:T(8,128)(2,1)} %m_ref.1, bf16[12,96,128]{2,1,0:T(8,128)(2,1)} %z_ref.1, s32[96,256]{1,0:T(8,128)} %bitcast.6, s32[1,96]{1,0:T(1,128)} %bitcast.11, bf16[256,1024]{1,0:T(8,128)(2,1)} %w_row_in.1, bf16[8,128]{1,0:T(8,128)(2,1)} %bitcast.8, ...), custom_call_target="tpu_custom_call" | custom-call | tf_op jit(solution)/shard_map/evoformer_block/pallas_call | solution.py:458
  136.7 0.0 copy-start
  136.7 2.7 %copy.21 = bf16[32,96,256]{2,1,0:T(8,128)(2,1)} copy(bf16[32,96,256]{2,1,0:T(8,128)(2,1)} %get-tuple-element.4) | data formatting | bytes 3145728
  139.4 0.0 copy-done
  139.4 0.7 copy.22
Async XLA Ops:
  136.7 2.7 %copy-start = (bf16[12,96,128]{2,1,0:T(8,128)(2,1)S(1)}, bf16[12,96,128]{2,1,0:T(8,128)(2,1)}, u32[]{:S(2)}) copy-start(bf16[12,96,128]{2,1,0:T(8,128)(2,1)} %get-tuple-element.5) | copy-start | bytes 884740

commit v3 on v2

--- a/solution.py
+++ b/solution.py
@@ -16,7 +16,6 @@
 HM, HT, HD, OPM = 8, 4, 32, 32
 LANES = 128
 MASKED = -1e9
-PADDED = -3e38
 SCALE = HD ** -0.5
 
 ROWB, MF, MB, STB, ZF, ENB, ZB = 0, 1, 5, 6, 7, 8, 9
@@ -60,53 +59,97 @@
     return (x.reshape(x.shape[0] // 16, 16, LANES) * mask[None]).reshape(x.shape)
 
 
-def softmax_rows(logits):
-    top = jnp.max(logits, axis=-1, keepdims=True)
-    weights = jnp.exp(logits - top)
-    return (weights * (1.0 / jnp.sum(weights, axis=-1, keepdims=True))).astype(BF16)
-
-
-def gate(tiles, g):
-    mixed = tiles[0] if len(tiles) == 1 else jnp.concatenate(tiles, axis=1)
-    return (mixed * jax.nn.sigmoid(g.astype(F32))).astype(BF16)
-
-
-def attend_padded(q, k, v, g, bias_ref, keep, heads):
+def dot_tl(a, b):
+    return lax.dot_general(a, b, (((0,), (0,)), ((), ())), preferred_element_type=F32)
+
+
+def softmax_keys(logits):
+    weights = jnp.exp(logits - jnp.max(logits, axis=0, keepdims=True))
+    return (weights * (1.0 / jnp.sum(weights, axis=0, keepdims=True))).astype(BF16)
+
+
+def pipeline(items, first, middle, last, finish):
+    opened, ready = {0: first(items[0])}, {}
+    for n in range(len(items) + 2):
+        if n + 1 < len(items):
+            opened[n + 1] = first(items[n + 1])
+        if n < len(items):
+            ready[n] = middle(items[n], opened.pop(n))
+        if 1 <= n <= len(items):
+            last(items[n - 1], ready.pop(n - 1))
+        if n >= 2:
+            finish(items[n - 2])
+
+
+def attend_biased(rows, tiles, q_of, k_of, vg_of, bias_ref, keep_of, w_out, store):
     masks = head_masks()
-    tiles = []
-    for t in range(heads // 4):
-        lanes = slice(t * LANES, (t + 1) * LANES)
-        probs = []
-        for pair in range(2):
-            kk = jnp.concatenate([only_head(k[:, lanes], masks[2 * pair + u]) for u in range(2)], axis=0)
-            scores = dot_t(q[:, lanes], kk)
-            for u in range(2):
-                logits = scores[:, u * LANES:(u + 1) * LANES] * SCALE + bias_ref[4 * t + 2 * pair + u]
-                probs.append(softmax_rows(jnp.where(keep, logits, MASKED)))
-        vv = jnp.concatenate([only_head(v[:, lanes], mask) for mask in masks], axis=0)
-        tiles.append(dot(jnp.concatenate(probs, axis=1), vv))
-    return gate(tiles, g)
-
-
-def attend_column(q, k, v, g, keep):
+    each = len(masks)
+    offsets = {u: (keep_of(u) - 1.0) * -MASKED for u in rows}
+    vgs = {}
+    mixed = {u: [] for u in rows}
+
+    def first(item):
+        u, t = item
+        if t == 0:
+            vgs[u] = vg_of(u)
+        k = k_of(u, t)
+        return dot_t(jnp.concatenate([only_head(k, mask) for mask in masks], axis=0), q_of(u, t))
+
+    def middle(item, scores):
+        u, t = item
+        return [softmax_keys((scores[n * RES:(n + 1) * RES] * SCALE + bias_ref[each * t + n]) * keep_of(u) + offsets[u])
+                for n in range(each)]
+
+    def last(item, probs):
+        u, t = item
+        for n in range(each):
+            h = each * t + n
+            mixed[u].append(dot(vgs[u][h * HD:(h + 1) * HD], probs[n]))
+
+    def finish(item):
+        u, t = item
+        if t == tiles - 1:
+            gates = jax.nn.sigmoid(vgs[u][tiles * LANES:].astype(F32))
+            store(u, dot_tl((jnp.concatenate(mixed[u], axis=0) * gates).astype(BF16), w_out))
+
+    pipeline([(u, t) for u in rows for t in range(tiles)], first, middle, last, finish)
+
+
+def attend_column(residues, q_of, k_of, vg_of, keep_of, w_out, store):
     masks = head_masks()
-    tiles = []
-    for t in range(HM // 4):
-        lanes = slice(t * LANES, (t + 1) * LANES)
-        probs = []
-        for mask in masks:
-            logits = dot_t(q[:, lanes], only_head(k[:, lanes], mask)) * SCALE
-            probs.append(softmax_rows(jnp.where(keep, logits, MASKED)))
-        vv = jnp.concatenate([only_head(v[:, lanes], mask) for mask in masks], axis=0)
-        tiles.append(dot(jnp.concatenate(probs, axis=1), vv))
-    return gate(tiles, g)
+    each = len(masks)
+    keeps, vgs = {}, {}
+    mixed = {u: [] for u in residues}
+
+    def first(item):
+        u, h = item
+        if h == 0:
+            keeps[u] = keep_of(u)
+            vgs[u] = vg_of(u)
+        return dot_t(only_head(k_of(u, h // each), masks[h % each]), q_of(u, h // each))
+
+    def middle(item, scores):
+        return softmax_keys(scores * (keeps[item[0]] * SCALE) + (keeps[item[0]] - 1.0) * -MASKED)
+
+    def last(item, probs):
+        u, h = item
+        mixed[u].append(dot(vgs[u][h * HD:(h + 1) * HD], probs))
+
+    def finish(item):
+        u, h = item
+        if h == HM - 1:
+            gates = jax.nn.sigmoid(vgs[u][CM:].astype(F32))
+            store(u, dot_tl((jnp.concatenate(mixed[u], axis=0) * gates).astype(BF16), w_out))
+
+    pipeline([(u, h) for u in residues for h in range(HM)], first, middle, last, finish)
 
 
 def block_kernel(m_ref, z_ref, mask_ref, res_ref, w_row_in, w_row_bias, w_row_out, w_col_in, w_col_out,
                  w_opm_in, w_opm_out, w_start_in, w_start_bias, w_start_out, w_end_in, w_end_bias, w_end_out,
                  m_out, z_out,
-                 perm, perm_out, perm_in, comp, hperm, keep_row, mask_t, norm, res_keep, wbt, bcol, bias,
-                 rowb_recv, stb_recv, enb_recv, proj, gated, projt, m1, msend, mcols, mback, colproj,
+                 perm, perm_out, perm_in, comp, hperm, keep_row, mask_t, mask_s, norm, res_keep, wbt, bcol, bias,
+                 rowb_recv, stb_recv, enb_recv, row_vg, col_vg, tri_vg, yrow, rowqk, triqk, m1, msend, mcols, mback,
+                 ycol, colqk,
                  left, crecv, cbig, outer, w2, w2t, ynorm, z1, zs, zr, z2, z3, zs2, zr2,
                  send_sem, recv_sem, local_sem, c_send, c_recv, c_pair):
     data = lax.axis_index('data')
@@ -156,6 +199,7 @@
     comp[...] = jnp.where(((c1 & 15) < RLOC) & (r1 == (c1 >> 4) * RLOC + (c1 & 15)), 1.0, 0.0).astype(BF16)
     r2, c2 = iota((LANES, LANES), 0), iota((LANES, LANES), 1)
     hperm[...] = jnp.where(((r2 >> 4) == (c2 & 7)) & ((r2 & 15) == (c2 >> 3)), 1.0, 0.0).astype(BF16)
+    eye = jnp.where(r2 == c2, 1.0, 0.0).astype(BF16)
     bcol[...] = jnp.zeros_like(bcol)
     wbt[...] = jnp.zeros_like(wbt)
     for n, w in enumerate((w_row_bias, w_start_bias, w_end_bias)):
@@ -178,9 +222,8 @@
 
     def take_bias(recv, heads, stage):
         wait_recv(stage, bias_rows(recv))
-        lane = iota((RES, LANES), 1)
         for h in range(heads):
-            bias[h] = jnp.where(lane < RES, dot(comp[...], recv[h]), PADDED)
+            bias[h] = dot_t(eye, dot(comp[...], recv[h]).astype(BF16))[0:RES]
 
     @pl.loop(0, RLOC)
     def _(i):
@@ -189,15 +232,23 @@
     pl.semaphore_wait(barrier, NDEV - 1)
     send_bias(rowb_recv, 0, HM, ROWB)
 
-    res_keep[...] = jnp.ones_like(res_keep)
-    res_keep[0:1, 0:RES] = res_ref[...]
-    eye = jnp.where(r2 == c2, 1.0, 0.0).astype(BF16)
-    eye256 = jnp.where(r0 == c0, 1.0, 0.0).astype(BF16)
+    res_keep[...] = dot((eye[0:RES, 0:RES].astype(F32) * res_ref[...].astype(F32)).astype(BF16),
+                        jnp.ones((RES, LANES), BF16))
     seq_order = jnp.where(r0 == ((c0 >> 3) & 7) * SLOC + (c0 >> 6) * CHUNK + (c0 & 7), 1.0, 0.0).astype(BF16)
+    seq_rows = jnp.where(c0 == ((r0 >> 3) & 7) * SLOC + (r0 >> 6) * CHUNK + (r0 & 7), 1.0, 0.0).astype(BF16)
     mt = mask_ref[...].astype(F32).astype(BF16)
-    keep_row[...] = jnp.ones_like(keep_row)
-    keep_row[:, 0:RES] = dot_t(eye256, mt)
     mask_t[...] = dot(mt, seq_order)
+    mask_s[...] = dot_t(seq_rows, mt).astype(BF16)
+
+    @pl.loop(0, SLOC)
+    def _(i):
+        pick = jnp.where(iota((SEQ, LANES), 0) == me * SLOC + i, 1.0, 0.0).astype(BF16)
+        keep_row[i] = dot(mask_ref[...].astype(F32).astype(BF16), pick)
+
+    row_vg[...] = jnp.transpose(w_row_in[:, 2 * CM:].astype(F32)).astype(BF16)
+    col_vg[...] = jnp.transpose(w_col_in[:, 2 * CM:].astype(F32)).astype(BF16)
+    tri_vg[0] = jnp.transpose(w_start_in[:, 2 * CZ:].astype(F32)).astype(BF16)
+    tri_vg[1] = jnp.transpose(w_end_in[:, 2 * CZ:].astype(F32)).astype(BF16)
     norm[...] = jnp.zeros_like(norm)
     norm[0:RES, 0:RES] = dot_t(mt, mt)
     w_full = w_opm_out[...].reshape(OPM, OPM, CZ)
@@ -206,8 +257,6 @@
             blk = w_full[16 * a:16 * a + 16, 16 * c:16 * c + 16, :].reshape(256, CZ)
             w2[16 * c:16 * c + 16, 16 * a:16 * a + 16, :] = dot(perm[...], blk).astype(BF16).reshape(16, 16, CZ)
     w2t[...] = dot_t(eye, w2[...].reshape(OPM * OPM, CZ)).astype(BF16)
-    proj[:, RES:, :] = jnp.zeros((proj.shape[0], LANES - RES, 4 * CM), BF16)
-    projt[:, RES:, :] = jnp.zeros((RLOC, LANES - RES, 4 * CZ), BF16)
     cbig[:, RES:, :] = jnp.zeros((OPM, LANES - RES, SEQ), BF16)
     z1[RLOC:, :, :] = jnp.zeros((16 - RLOC, RES, CZ), BF16)
     z3[RLOC:, :, :] = jnp.zeros((16 - RLOC, RES, CZ), BF16)
@@ -228,13 +277,17 @@
         def _(blk):
             s0 = q * CHUNK + blk * 4
             x = m_ref[pl.ds(s0, 4)].reshape(4 * RES, CM)
-            proj[:, 0:RES, :] = dot(layer_norm(x), w_row_in[...]).astype(BF16).reshape(4, RES, 4 * CM)
-            for u in range(4):
-                keep = keep_row[pl.ds(me * SLOC + s0 + u, 1), :] != 0.0
-                gated[u] = attend_padded(proj[u, 0:RES, 0:CM], proj[u, :, CM:2 * CM], proj[u, :, 2 * CM:3 * CM],
-                                         proj[u, 0:RES, 3 * CM:4 * CM], bias, keep, HM)
-            update = dot(gated[...].reshape(4 * RES, CM), w_row_out[...])
-            m1[pl.ds(s0, 4)] = add_residual(x, update).reshape(4, RES, CM)
+            y = layer_norm(x)
+            yrow[...] = y.reshape(4, RES, CM)
+            qk = dot(y, w_row_in[:, 0:2 * CM]).astype(BF16)
+            for t in range(4):
+                rowqk[t] = qk[:, t * LANES:(t + 1) * LANES].reshape(4, RES, LANES)
+
+            def store(u, update):
+                m1[s0 + u] = add_residual(m_ref[s0 + u], update)
+            attend_biased(range(4), 2, lambda u, t: rowqk[t, u], lambda u, t: rowqk[2 + t, u],
+                          lambda u: dot_t(row_vg[...], yrow[u]).astype(BF16), bias,
+                          lambda u: keep_row[s0 + u, :, 0:RES], w_row_out[...], store)
 
         for j in range(RES // 32):
             blk = m1[CHUNK * q:CHUNK * q + CHUNK, 32 * j:32 * j + 32, :].reshape(256, CM)
@@ -249,8 +302,12 @@
         @pl.loop(0, RLOC // 4)
         def _(blk):
             x = mcols[q, pl.ds(blk * 4, 4)].reshape(4 * CROWS, CM)
-            y = dot(layer_norm(x), w_col_in[...]).astype(BF16).reshape(4, CROWS, 4 * CM)
-            colproj[pl.ds(blk * 4, 4), CROWS * q:CROWS * q + CROWS, :] = y
+            y = layer_norm(x)
+            ycol[pl.ds(blk * 4, 4), CROWS * q:CROWS * q + CROWS, :] = y.reshape(4, CROWS, CM)
+            qk = dot(y, w_col_in[:, 0:2 * CM]).astype(BF16)
+            for t in range(4):
+                colqk[t, pl.ds(blk * 4, 4), CROWS * q:CROWS * q + CROWS, :] = (
+                    qk[:, t * LANES:(t + 1) * LANES].reshape(4, CROWS, LANES))
 
     row_chunk(0)
     row_chunk(1)
@@ -271,29 +328,40 @@
             remote(row, row, c_send.at[t], c_recv.at[t, j], twin).wait_recv()
             remote(row, row, c_send.at[3 + t], c_pair.at[t], partner).start()
 
-    @pl.loop(0, RLOC)
-    def _(j):
-        x = mcols[:, j].reshape(SEQ, CM)
-        mask_row = mask_t[pl.ds(me * RLOC + j, 1), :]
-        mixed = attend_column(colproj[j, :, 0:CM], colproj[j, :, CM:2 * CM], colproj[j, :, 2 * CM:3 * CM],
-                              colproj[j, :, 3 * CM:], mask_row != 0.0)
-        x = add_residual(x, dot(mixed, w_col_out[...]))
-        both = dot_t(w_opm_in[...], layer_norm(x)).astype(BF16).astype(F32) * mask_row
-        left[j] = both[0:OPM].astype(BF16)
-        crecv[me * RLOC + j] = both[OPM:].astype(BF16)
-        row = crecv.at[me * RLOC + j]
-        for t, twin in enumerate(twins):
-            remote(row, row, c_send.at[t], c_recv.at[t, j], twin).start()
-        remote(row, row, c_send.at[6], c_pair.at[3], partner).start()
-        mcols[:, j] = x.reshape(NCHUNK, CROWS, CM)
-
-        @pl.when(j >= LAG)
+    @pl.loop(0, RLOC // 2)
+    def _(pair):
+        def keep_of(u):
+            pick = jnp.where(iota((RES, LANES), 0) == me * RLOC + pair * 2 + u, 1.0, 0.0).astype(BF16)
+            keep = dot(mask_s[...], pick)
+            return jnp.concatenate([keep, keep], axis=1)
+
+        def store(u, update):
+            j = pair * 2 + u
+            mask_row = mask_t[pl.ds(me * RLOC + j, 1), :]
+            x = add_residual(mcols[:, j].reshape(SEQ, CM), update)
+            both = dot_t(w_opm_in[...], layer_norm(x)).astype(BF16).astype(F32) * mask_row
+            left[j] = both[0:OPM].astype(BF16)
+            crecv[me * RLOC + j] = both[OPM:].astype(BF16)
+            mcols[:, j] = x.reshape(NCHUNK, CROWS, CM)
+
+        attend_column(range(2), lambda u, t: colqk[t, pair * 2 + u], lambda u, t: colqk[2 + t, pair * 2 + u],
+                      lambda u: dot_t(col_vg[...], ycol[pair * 2 + u]).astype(BF16), keep_of, w_col_out[...], store)
+        for u in range(2):
+            j = pair * 2 + u
+            row = crecv.at[me * RLOC + j]
+            for t, twin in enumerate(twins):
+                remote(row, row, c_send.at[t], c_recv.at[t, j], twin).start()
+            remote(row, row, c_send.at[6], c_pair.at[3], partner).start()
+
+        @pl.when(pair >= 1)
         def _():
-            relay(j - LAG)
-
-        @pl.when(j < MB_EARLY)
+            for u in range(2):
+                relay(pair * 2 - 2 + u)
+
+        @pl.when(pair < MB_EARLY // 2)
         def _():
-            mb_start(j)
+            for u in range(2):
+                mb_start(pair * 2 + u)
 
     for j in range(RLOC - LAG, RLOC):
         relay(j)
@@ -337,23 +405,20 @@
         @pl.loop(0, RLOC // 4)
         def _(blk):
             y = ynorm[pl.ds(blk * 4, 4)].reshape(4 * RES, CZ)
-            projt[pl.ds(blk * 4, 4), 0:RES, :] = dot(y, w_in[...]).astype(BF16).reshape(4, RES, 4 * CZ)
+            qk = dot(y, w_in[:, 0:2 * CZ]).astype(BF16)
+            for t in range(2):
+                triqk[t, pl.ds(blk * 4, 4)] = qk[:, t * LANES:(t + 1) * LANES].reshape(4, RES, LANES)
         take_bias(recv, HT, stage)
         for j in late:
             mb_start(j)
-        keep = res_keep[0:1, :] != 0
 
         @pl.loop(0, RLOC // 4)
         def _(blk):
-            i0 = blk * 4
-            for u in range(4):
-                i = i0 + u
-                gated[u, :, 0:CZ] = attend_padded(projt[i, 0:RES, 0:CZ], projt[i, :, CZ:2 * CZ],
-                                                  projt[i, :, 2 * CZ:3 * CZ], projt[i, 0:RES, 3 * CZ:4 * CZ],
-                                                  bias, keep, HT)
-            update = dot(gated[:, :, 0:CZ].reshape(4 * RES, CZ), w_out[...])
-            x = state[pl.ds(i0, 4)].reshape(4 * RES, CZ)
-            result[pl.ds(i0, 4)] = add_residual(x, update).reshape(4, RES, CZ)
+            def store(u, update):
+                result[blk * 4 + u] = add_residual(state[blk * 4 + u], update)
+            attend_biased(range(4), 1, lambda u, t: triqk[0, blk * 4 + u], lambda u, t: triqk[1, blk * 4 + u],
+                          lambda u: dot_t(tri_vg[which - 1], ynorm[blk * 4 + u]).astype(BF16), bias,
+                          lambda u: res_keep[:, 0:RES], w_out[...], store)
 
     def z_src(buf):
         return lambda d: buf.at[pl.ds(d * RLOC, RLOC)]
@@ -416,24 +481,29 @@
             pltpu.VMEM((256, 256), BF16),
             pltpu.VMEM((RES, LANES), BF16),
             pltpu.VMEM((LANES, LANES), BF16),
-            pltpu.VMEM((SEQ, LANES), F32),
+            pltpu.VMEM((SLOC, RES, LANES), F32),
             pltpu.VMEM((RES, SEQ), F32),
+            pltpu.VMEM((SEQ, RES), BF16),
             pltpu.VMEM((LANES, LANES), F32),
-            pltpu.VMEM((8, LANES), jnp.int32),
+            pltpu.VMEM((RES, LANES), F32),
             pltpu.VMEM((3, 8, CZ), F32),
             pltpu.VMEM((16, 8, LANES), F32),
-            pltpu.VMEM((HM, RES, LANES), F32),
+            pltpu.VMEM((HM, RES, RES), F32),
             pltpu.VMEM((HM, LANES, LANES), BF16),
             pltpu.VMEM((HT, LANES, LANES), BF16),
             pltpu.VMEM((HT, LANES, LANES), BF16),
-            pltpu.VMEM((4, LANES, 4 * CM), BF16),
+            pltpu.VMEM((2 * CM, CM), BF16),
+            pltpu.VMEM((2 * CM, CM), BF16),
+            pltpu.VMEM((2, 2 * CZ, CZ), BF16),
             pltpu.VMEM((4, RES, CM), BF16),
-            pltpu.VMEM((RLOC, LANES, 4 * CZ), BF16),
+            pltpu.VMEM((4, 4, RES, LANES), BF16),
+            pltpu.VMEM((2, RLOC, RES, LANES), BF16),
             pltpu.VMEM((SLOC, RES, CM), BF16),
             pltpu.VMEM((NCHUNK, RES, CHUNK, CM), BF16),
             pltpu.VMEM((NCHUNK, RLOC, CROWS, CM), BF16),
             pltpu.VMEM((NCHUNK, RES * CHUNK, CM), BF16),
-            pltpu.VMEM((RLOC, SEQ, 4 * CM), BF16),
+            pltpu.VMEM((RLOC, SEQ, CM), BF16),
+            pltpu.VMEM((4, RLOC, SEQ, LANES), BF16),
             pltpu.VMEM((RLOC, OPM, SEQ), BF16),
             pltpu.VMEM((RES, OPM, SEQ), BF16),
             pltpu.VMEM((OPM, LANES, SEQ), BF16),

time: 140 us -> 124 us (0.89)
  Pallas kernels: 136 us -> 119 us
    pallas_call x1, Pallas kernels: 136 us -> 119 us  [per_device(): pl.pallas_call(block_kernel, name='evoformer_block', out_shape=(jax.Shape...]
where the time goes in v3:
time: 124 us; the launch traced here: 123 us
  Pallas kernels  119 us (96%)
  local copies, waits for them, and re-layouts  3.41 us (3%)
    pallas_call x1, Pallas kernels, per_device(): pl.pallas_call(block_kernel, name='evoformer_block', out_shape=(jax.Shape...  119 us
    unnamed x4, local copies, waits for them, and re-layouts  3.41 us

profile of v3, /device:TPU:0, one launch (start us, length us, event | category | flops | bytes accessed | tf_op | source)
XLA Modules:
  0.0 123.4 jit_solution(9230507793779687152)
XLA Ops:
  0.6 119.3 %evoformer_block.1 = (bf16[32,96,256]{2,1,0:T(8,128)(2,1)}, bf16[12,96,128]{2,1,0:T(8,128)(2,1)}) custom-call(bf16[32,96,256]{2,1,0:T(8,128)(2,1)} %m_ref.1, bf16[12,96,128]{2,1,0:T(8,128)(2,1)} %z_ref.1, s32[96,256]{1,0:T(8,128)} %bitcast.6, s32[1,96]{1,0:T(1,128)} %bitcast.11, bf16[256,1024]{1,0:T(8,128)(2,1)} %w_row_in.1, bf16[8,128]{1,0:T(8,128)(2,1)} %bitcast.8, ...), custom_call_target="tpu_custom_call" | custom-call | tf_op jit(solution)/shard_map/evoformer_block/pallas_call | solution.py:528
  119.9 0.0 copy-start
  120.0 2.7 %copy.21 = bf16[32,96,256]{2,1,0:T(8,128)(2,1)} copy(bf16[32,96,256]{2,1,0:T(8,128)(2,1)} %get-tuple-element.4) | data formatting | bytes 3145728
  122.7 0.0 copy-done
  122.7 0.7 copy.22
Async XLA Ops:
  119.9 2.7 %copy-start = (bf16[12,96,128]{2,1,0:T(8,128)(2,1)S(1)}, bf16[12,96,128]{2,1,0:T(8,128)(2,1)}, u32[]{:S(2)}) copy-start(bf16[12,96,128]{2,1,0:T(8,128)(2,1)} %get-tuple-element.5) | copy-start | bytes 884740

commit v4 on v3

--- a/solution.py
+++ b/solution.py
@@ -17,6 +17,7 @@
 LANES = 128
 MASKED = -1e9
 SCALE = HD ** -0.5
+LOG2E = 1.4426950408889634
 
 ROWB, MF, MB, STB, ZF, ENB, ZB = 0, 1, 5, 6, 7, 8, 9
 NSTAGE = 10
@@ -56,15 +57,15 @@
 
 
 def only_head(x, mask):
-    return (x.reshape(x.shape[0] // 16, 16, LANES) * mask[None]).reshape(x.shape)
+    return x * jnp.concatenate([mask] * (x.shape[0] // 16), axis=0)
 
 
 def dot_tl(a, b):
     return lax.dot_general(a, b, (((0,), (0,)), ((), ())), preferred_element_type=F32)
 
 
-def softmax_keys(logits):
-    weights = jnp.exp(logits - jnp.max(logits, axis=0, keepdims=True))
+def softmax_keys(logits, exponential=jnp.exp):
+    weights = exponential(logits - jnp.max(logits, axis=0, keepdims=True))
     return (weights * (1.0 / jnp.sum(weights, axis=0, keepdims=True))).astype(BF16)
 
 
@@ -104,7 +105,8 @@
         u, t = item
         for n in range(each):
             h = each * t + n
-            mixed[u].append(dot(vgs[u][h * HD:(h + 1) * HD], probs[n]))
+            padded = jnp.concatenate([probs[n], jnp.zeros((LANES - RES, LANES), BF16)], axis=0)
+            mixed[u].append(dot(vgs[u][h * HD:(h + 1) * HD], padded))
 
     def finish(item):
         u, t = item
@@ -129,7 +131,8 @@
         return dot_t(only_head(k_of(u, h // each), masks[h % each]), q_of(u, h // each))
 
     def middle(item, scores):
-        return softmax_keys(scores * (keeps[item[0]] * SCALE) + (keeps[item[0]] - 1.0) * -MASKED)
+        keep = keeps[item[0]]
+        return softmax_keys(scores * (keep * (SCALE * LOG2E)) + (keep - 1.0) * (-MASKED * LOG2E), jnp.exp2)
 
     def last(item, probs):
         u, h = item
@@ -148,7 +151,7 @@
                  w_opm_in, w_opm_out, w_start_in, w_start_bias, w_start_out, w_end_in, w_end_bias, w_end_out,
                  m_out, z_out,
                  perm, perm_out, perm_in, comp, hperm, keep_row, mask_t, mask_s, norm, res_keep, wbt, bcol, bias,
-                 rowb_recv, stb_recv, enb_recv, row_vg, col_vg, tri_vg, yrow, rowqk, triqk, m1, msend, mcols, mback,
+                 rowb_recv, stb_recv, enb_recv, row_vg, col_vg, tri_vg, yrow, rowqk, triqk, m1, msend, mrecv, mcols, mdone, mback,
                  ycol, colqk,
                  left, crecv, cbig, outer, w2, w2t, ynorm, z1, zs, zr, z2, z3, zs2, zr2,
                  send_sem, recv_sem, local_sem, c_send, c_recv, c_pair):
@@ -210,24 +213,26 @@
 
         @pl.loop(0, RLOC)
         def _(i):
-            bcol[i, :, 0:RES] = dot_t(weights, ynorm[i])
+            bcol[i] = dot_t(weights, ynorm[i])
 
         mine = dot(hperm[0:heads * 16, :], bcol[...].reshape(LANES, LANES).astype(BF16)).astype(BF16)
-        rows = pl.ds(pl.multiple_of(me * 16, 16), 16)
-        recv[:, rows, :] = mine.reshape(heads, 16, LANES)
-        start_all(stage, lambda d: recv.at[:, rows, :], lambda s: recv.at[:, rows, :])
+        recv[me] = mine.reshape(heads, 16, LANES)
+        start_all(stage, lambda d: recv.at[me], lambda s: recv.at[s])
 
     def bias_rows(recv):
-        return lambda s: recv.at[:, pl.ds(pl.multiple_of(s * 16, 16), 16), :]
+        return lambda s: recv.at[s]
 
     def take_bias(recv, heads, stage):
         wait_recv(stage, bias_rows(recv))
         for h in range(heads):
-            bias[h] = dot_t(eye, dot(comp[...], recv[h]).astype(BF16))[0:RES]
+            rows = dot(comp[...], recv[:, h].reshape(LANES, LANES)).astype(BF16)
+            bias[h] = dot_t(eye, jnp.concatenate([rows, jnp.zeros((LANES - RES, LANES), BF16)], axis=0))[0:RES]
+
+    ynorm[:, RES:, :] = jnp.zeros((RLOC, LANES - RES, CZ), BF16)
 
     @pl.loop(0, RLOC)
     def _(i):
-        ynorm[i] = layer_norm(z_ref[i])
+        ynorm[i, 0:RES, :] = layer_norm(z_ref[i])
 
     pl.semaphore_wait(barrier, NDEV - 1)
     send_bias(rowb_recv, 0, HM, ROWB)
@@ -245,10 +250,10 @@
         pick = jnp.where(iota((SEQ, LANES), 0) == me * SLOC + i, 1.0, 0.0).astype(BF16)
         keep_row[i] = dot(mask_ref[...].astype(F32).astype(BF16), pick)
 
-    row_vg[...] = jnp.transpose(w_row_in[:, 2 * CM:].astype(F32)).astype(BF16)
-    col_vg[...] = jnp.transpose(w_col_in[:, 2 * CM:].astype(F32)).astype(BF16)
-    tri_vg[0] = jnp.transpose(w_start_in[:, 2 * CZ:].astype(F32)).astype(BF16)
-    tri_vg[1] = jnp.transpose(w_end_in[:, 2 * CZ:].astype(F32)).astype(BF16)
+    row_vg[...] = jnp.transpose(w_row_in[:, 2 * CM:])
+    col_vg[...] = jnp.transpose(w_col_in[:, 2 * CM:])
+    tri_vg[0] = jnp.transpose(w_start_in[:, 2 * CZ:])
+    tri_vg[1] = jnp.transpose(w_end_in[:, 2 * CZ:])
     norm[...] = jnp.zeros_like(norm)
     norm[0:RES, 0:RES] = dot_t(mt, mt)
     w_full = w_opm_out[...].reshape(OPM, OPM, CZ)
@@ -258,6 +263,9 @@
             w2[16 * c:16 * c + 16, 16 * a:16 * a + 16, :] = dot(perm[...], blk).astype(BF16).reshape(16, 16, CZ)
     w2t[...] = dot_t(eye, w2[...].reshape(OPM * OPM, CZ)).astype(BF16)
     cbig[:, RES:, :] = jnp.zeros((OPM, LANES - RES, SEQ), BF16)
+    yrow[:, RES:, :] = jnp.zeros((4, LANES - RES, CM), BF16)
+    rowqk[:, :, RES:, :] = jnp.zeros((4, 4, LANES - RES, LANES), BF16)
+    triqk[:, :, RES:, :] = jnp.zeros((2, RLOC, LANES - RES, LANES), BF16)
     z1[RLOC:, :, :] = jnp.zeros((16 - RLOC, RES, CZ), BF16)
     z3[RLOC:, :, :] = jnp.zeros((16 - RLOC, RES, CZ), BF16)
 
@@ -267,7 +275,7 @@
         return lambda d: msend.at[q, pl.ds(d * RLOC, RLOC)]
 
     def m_dst(q):
-        return lambda s: mcols.at[q, :, pl.ds(pl.multiple_of(s * CHUNK, CHUNK), CHUNK), :]
+        return lambda s: mrecv.at[q, s]
 
     def local_copy(src, dst, n):
         return pltpu.make_async_copy(src, dst, local_sem.at[n])
@@ -278,16 +286,16 @@
             s0 = q * CHUNK + blk * 4
             x = m_ref[pl.ds(s0, 4)].reshape(4 * RES, CM)
             y = layer_norm(x)
-            yrow[...] = y.reshape(4, RES, CM)
+            yrow[:, 0:RES, :] = y.reshape(4, RES, CM)
             qk = dot(y, w_row_in[:, 0:2 * CM]).astype(BF16)
             for t in range(4):
-                rowqk[t] = qk[:, t * LANES:(t + 1) * LANES].reshape(4, RES, LANES)
+                rowqk[t, :, 0:RES, :] = qk[:, t * LANES:(t + 1) * LANES].reshape(4, RES, LANES)
 
             def store(u, update):
-                m1[s0 + u] = add_residual(m_ref[s0 + u], update)
-            attend_biased(range(4), 2, lambda u, t: rowqk[t, u], lambda u, t: rowqk[2 + t, u],
+                m1[s0 + u] = add_residual(m_ref[s0 + u], update[0:RES])
+            attend_biased(range(4), 2, lambda u, t: rowqk[t, u], lambda u, t: rowqk[2 + t, u, 0:RES],
                           lambda u: dot_t(row_vg[...], yrow[u]).astype(BF16), bias,
-                          lambda u: keep_row[s0 + u, :, 0:RES], w_row_out[...], store)
+                          lambda u: keep_row[s0 + u], w_row_out[...], store)
 
         for j in range(RES // 32):
             blk = m1[CHUNK * q:CHUNK * q + CHUNK, 32 * j:32 * j + 32, :].reshape(256, CM)
@@ -301,7 +309,9 @@
 
         @pl.loop(0, RLOC // 4)
         def _(blk):
-            x = mcols[q, pl.ds(blk * 4, 4)].reshape(4 * CROWS, CM)
+            x = jnp.concatenate([mrecv[q, :, blk * 4 + u].astype(F32).reshape(CROWS, CM) for u in range(4)], axis=0)
+            for u in range(4):
+                mcols[q, blk * 4 + u] = x[u * CROWS:(u + 1) * CROWS].astype(BF16)
             y = layer_norm(x)
             ycol[pl.ds(blk * 4, 4), CROWS * q:CROWS * q + CROWS, :] = y.reshape(4, CROWS, CM)
             qk = dot(y, w_col_in[:, 0:2 * CM]).astype(BF16)
@@ -319,8 +329,7 @@
     column_projection(3)
 
     def mb_start(j):
-        start_all(MB, lambda d: mcols.at[:, j, pl.ds(pl.multiple_of(d * CHUNK, CHUNK), CHUNK), :],
-                  lambda s: mback.at[:, pl.ds(pl.multiple_of((s * RLOC + j) * CHUNK, CHUNK), CHUNK), :])
+        start_all(MB, lambda d: mdone.at[d, j], lambda s: mback.at[s * RLOC + j])
 
     def relay(j):
         for t, twin in enumerate(twins):
@@ -342,7 +351,9 @@
             both = dot_t(w_opm_in[...], layer_norm(x)).astype(BF16).astype(F32) * mask_row
             left[j] = both[0:OPM].astype(BF16)
             crecv[me * RLOC + j] = both[OPM:].astype(BF16)
-            mcols[:, j] = x.reshape(NCHUNK, CROWS, CM)
+            done = x.astype(F32).reshape(NCHUNK, NDEV, CHUNK, CM).astype(BF16)
+            for d in range(NDEV):
+                mdone[d, j] = done[:, d]
 
         attend_column(range(2), lambda u, t: colqk[t, pair * 2 + u], lambda u, t: colqk[2 + t, pair * 2 + u],
                       lambda u: dot_t(col_vg[...], ycol[pair * 2 + u]).astype(BF16), keep_of, w_col_out[...], store)
@@ -365,9 +376,7 @@
 
     for j in range(RLOC - LAG, RLOC):
         relay(j)
-    for q in range(NCHUNK):
-        mine = mcols[q, :, pl.ds(pl.multiple_of(me * CHUNK, CHUNK), CHUNK), :]
-        mback[q, pl.ds(pl.multiple_of(me * (RLOC * CHUNK), 32), RLOC * CHUNK), :] = mine.reshape(RLOC * CHUNK, CM)
+    mback[pl.ds(me * RLOC, RLOC)] = mdone[me]
 
     def c_rows(s):
         return crecv.at[pl.ds(s * RLOC, RLOC)]
@@ -399,15 +408,15 @@
     def triangle(state, result, w_in, which, w_out, recv, stage, late):
         @pl.loop(0, RLOC)
         def _(i):
-            ynorm[i] = layer_norm(state[i])
+            ynorm[i, 0:RES, :] = layer_norm(state[i])
         send_bias(recv, which, HT, stage)
 
         @pl.loop(0, RLOC // 4)
         def _(blk):
-            y = ynorm[pl.ds(blk * 4, 4)].reshape(4 * RES, CZ)
+            y = ynorm[pl.ds(blk * 4, 4), 0:RES, :].reshape(4 * RES, CZ)
             qk = dot(y, w_in[:, 0:2 * CZ]).astype(BF16)
             for t in range(2):
-                triqk[t, pl.ds(blk * 4, 4)] = qk[:, t * LANES:(t + 1) * LANES].reshape(4, RES, LANES)
+                triqk[t, pl.ds(blk * 4, 4), 0:RES, :] = qk[:, t * LANES:(t + 1) * LANES].reshape(4, RES, LANES)
         take_bias(recv, HT, stage)
         for j in late:
             mb_start(j)
@@ -415,16 +424,16 @@
         @pl.loop(0, RLOC // 4)
         def _(blk):
             def store(u, update):
-                result[blk * 4 + u] = add_residual(state[blk * 4 + u], update)
-            attend_biased(range(4), 1, lambda u, t: triqk[0, blk * 4 + u], lambda u, t: triqk[1, blk * 4 + u],
+                result[blk * 4 + u] = add_residual(state[blk * 4 + u], update[0:RES])
+            attend_biased(range(4), 1, lambda u, t: triqk[0, blk * 4 + u], lambda u, t: triqk[1, blk * 4 + u, 0:RES],
                           lambda u: dot_t(tri_vg[which - 1], ynorm[blk * 4 + u]).astype(BF16), bias,
-                          lambda u: res_keep[:, 0:RES], w_out[...], store)
+                          lambda u: res_keep[...], w_out[...], store)
 
     def z_src(buf):
         return lambda d: buf.at[pl.ds(d * RLOC, RLOC)]
 
     def z_dst(buf):
-        return lambda s: buf.at[:, pl.ds(pl.multiple_of(s * 16, 16), 16), :]
+        return lambda s: buf.at[s]
 
     def exchange(state, send, recv, result, stage, n):
         for j in range(RES // 16):
@@ -438,7 +447,7 @@
 
         @pl.loop(0, RLOC)
         def _(i):
-            result[i] = dot(comp[...], recv[i]).astype(BF16)
+            result[i] = dot(comp[...], recv[:, i].reshape(LANES, CZ)).astype(BF16)
 
     triangle(z1, z1, w_start_in, 1, w_start_out, stb_recv, STB, (MB_EARLY + 3, MB_EARLY + 4))
     exchange(z1, zs, zr, z2, ZF, NCHUNK)
@@ -446,19 +455,19 @@
     exchange(z3, zs2, zr2, z_out, ZB, NCHUNK + 1)
 
     def mb_dst(s):
-        return mback.at[:, pl.ds(pl.multiple_of(s * (RLOC * CHUNK), 32), RLOC * CHUNK), :]
+        return mback.at[pl.ds(s * RLOC, RLOC)]
     wait_recv(MB, mb_dst)
     for q in range(NCHUNK):
         @pl.loop(0, RES // 32)
         def _(j):
-            blk = mback[q, pl.ds(pl.multiple_of(j * 256, 256), 256), :]
+            blk = mback[pl.ds(j * 32, 32), q].astype(F32).reshape(256, CM).astype(BF16)
             rows = dot(perm_in[...], blk).astype(BF16).reshape(CHUNK, 32, CM)
             m_out[CHUNK * q:CHUNK * q + CHUNK, pl.ds(pl.multiple_of(j * 32, 32), 32), :] = rows
 
     wait_send(ROWB, lambda d: bias_rows(rowb_recv)(me))
     for q in range(NCHUNK):
         wait_send(MF + q, m_src(q))
-    wait_send(MB, lambda d: mcols.at[:, :, pl.ds(pl.multiple_of(d * CHUNK, CHUNK), CHUNK), :])
+    wait_send(MB, lambda d: mdone.at[d])
     for t in range(7):
         rows = c_rows(me if t in (0, 1, 2, 6) else twins[t - 3])
         remote(rows, rows, c_send.at[t], c_pair.at[0], partner).wait_send()
@@ -488,20 +497,22 @@
             pltpu.VMEM((RES, LANES), F32),
             pltpu.VMEM((3, 8, CZ), F32),
             pltpu.VMEM((16, 8, LANES), F32),
-            pltpu.VMEM((HM, RES, RES), F32),
-            pltpu.VMEM((HM, LANES, LANES), BF16),
-            pltpu.VMEM((HT, LANES, LANES), BF16),
-            pltpu.VMEM((HT, LANES, LANES), BF16),
+            pltpu.VMEM((HM, RES, LANES), F32),
+            pltpu.VMEM((NDEV, HM, 16, LANES), BF16),
+            pltpu.VMEM((NDEV, HT, 16, LANES), BF16),
+            pltpu.VMEM((NDEV, HT, 16, LANES), BF16),
             pltpu.VMEM((2 * CM, CM), BF16),
             pltpu.VMEM((2 * CM, CM), BF16),
             pltpu.VMEM((2, 2 * CZ, CZ), BF16),
-            pltpu.VMEM((4, RES, CM), BF16),
-            pltpu.VMEM((4, 4, RES, LANES), BF16),
-            pltpu.VMEM((2, RLOC, RES, LANES), BF16),
+            pltpu.VMEM((4, LANES, CM), BF16),
+            pltpu.VMEM((4, 4, LANES, LANES), BF16),
+            pltpu.VMEM((2, RLOC, LANES, LANES), BF16),
             pltpu.VMEM((SLOC, RES, CM), BF16),
             pltpu.VMEM((NCHUNK, RES, CHUNK, CM), BF16),
+            pltpu.VMEM((NCHUNK, NDEV, RLOC, CHUNK, CM), BF16),
             pltpu.VMEM((NCHUNK, RLOC, CROWS, CM), BF16),
-            pltpu.VMEM((NCHUNK, RES * CHUNK, CM), BF16),
+            pltpu.VMEM((NDEV, RLOC, NCHUNK, CHUNK, CM), BF16),
+            pltpu.VMEM((RES, NCHUNK, CHUNK, CM), BF16),
             pltpu.VMEM((RLOC, SEQ, CM), BF16),
             pltpu.VMEM((4, RLOC, SEQ, LANES), BF16),
             pltpu.VMEM((RLOC, OPM, SEQ), BF16),
@@ -510,14 +521,14 @@
             pltpu.VMEM((RLOC, OPM, OPM, LANES), BF16),
             pltpu.VMEM((OPM, OPM, CZ), BF16),
             pltpu.VMEM((CZ, OPM * OPM), BF16),
+            pltpu.VMEM((RLOC, LANES, CZ), BF16),
+            pltpu.VMEM((16, RES, CZ), BF16),
+            pltpu.VMEM((RES, 16, CZ), BF16),
+            pltpu.VMEM((NDEV, RLOC, 16, CZ), BF16),
             pltpu.VMEM((RLOC, RES, CZ), BF16),
             pltpu.VMEM((16, RES, CZ), BF16),
             pltpu.VMEM((RES, 16, CZ), BF16),
-            pltpu.VMEM((RLOC, LANES, CZ), BF16),
-            pltpu.VMEM((RLOC, RES, CZ), BF16),
-            pltpu.VMEM((16, RES, CZ), BF16),
-            pltpu.VMEM((RES, 16, CZ), BF16),
-            pltpu.VMEM((RLOC, LANES, CZ), BF16),
+            pltpu.VMEM((NDEV, RLOC, 16, CZ), BF16),
             pltpu.SemaphoreType.DMA((NSTAGE, NDEV)),
             pltpu.SemaphoreType.DMA((NSTAGE, NDEV)),
             pltpu.SemaphoreType.DMA((NCHUNK + 2,)),

time: 124 us -> 123 us (level)
  no operation moved by 1% of the time
where the time goes in v4:
time: 123 us
  Pallas kernels  119 us (97%)
  local copies, waits for them, and re-layouts  3.41 us (3%)
    pallas_call x1, Pallas kernels, per_device(): pl.pallas_call(block_kernel, name='evoformer_block', out_shape=(jax.Shape...  119 us
    unnamed x4, local copies, waits for them, and re-layouts  3.41 us

profile of v4, /device:TPU:0, one launch (start us, length us, event | category | flops | bytes accessed | tf_op | source)
XLA Modules:
  0.0 123.3 jit_solution(681480730476317109)
XLA Ops:
  0.6 119.2 %evoformer_block.1 = (bf16[32,96,256]{2,1,0:T(8,128)(2,1)}, bf16[12,96,128]{2,1,0:T(8,128)(2,1)}) custom-call(bf16[32,96,256]{2,1,0:T(8,128)(2,1)} %m_ref.1, bf16[12,96,128]{2,1,0:T(8,128)(2,1)} %z_ref.1, s32[96,256]{1,0:T(8,128)} %bitcast.6, s32[1,96]{1,0:T(1,128)} %bitcast.11, bf16[256,1024]{1,0:T(8,128)(2,1)} %w_row_in.1, bf16[8,128]{1,0:T(8,128)(2,1)} %bitcast.8, ...), custom_call_target="tpu_custom_call" | custom-call | tf_op jit(solution)/shard_map/evoformer_block/pallas_call | solution.py:539
  119.9 0.0 copy-start
  119.9 2.7 %copy.21 = bf16[32,96,256]{2,1,0:T(8,128)(2,1)} copy(bf16[32,96,256]{2,1,0:T(8,128)(2,1)} %get-tuple-element.4) | data formatting | bytes 3145728
  122.6 0.0 copy-done
  122.6 0.7 copy.22
Async XLA Ops:
  119.9 2.7 %copy-start = (bf16[12,96,128]{2,1,0:T(8,128)(2,1)S(1)}, bf16[12,96,128]{2,1,0:T(8,128)(2,1)}, u32[]{:S(2)}) copy-start(bf16[12,96,128]{2,1,0:T(8,128)(2,1)} %get-tuple-element.5) | copy-start | bytes 884740

commit v5 on v4

--- a/solution.py
+++ b/solution.py
@@ -19,13 +19,14 @@
 SCALE = HD ** -0.5
 LOG2E = 1.4426950408889634
 
-ROWB, MF, MB, STB, ZF, ENB, ZB = 0, 1, 5, 6, 7, 8, 9
-NSTAGE = 10
+ROWB, MF, MB, STB, ZF, ENB, ZB = 0, 1, 5, 6, 7, 9, 10
+NSTAGE = 12
+ZGROUP = RLOC // 2
 CHUNK = 8
 NCHUNK = SLOC // CHUNK
 CROWS = NDEV * CHUNK
 LAG = 2
-MB_EARLY = 6
+MB_EARLY = 8
 
 
 def dot(a, b):
@@ -147,14 +148,15 @@
     pipeline([(u, h) for u in residues for h in range(HM)], first, middle, last, finish)
 
 
-def block_kernel(m_ref, z_ref, mask_ref, res_ref, w_row_in, w_row_bias, w_row_out, w_col_in, w_col_out,
-                 w_opm_in, w_opm_out, w_start_in, w_start_bias, w_start_out, w_end_in, w_end_bias, w_end_out,
-                 m_out, z_out,
-                 perm, perm_out, perm_in, comp, hperm, keep_row, mask_t, mask_s, norm, res_keep, wbt, bcol, bias,
-                 rowb_recv, stb_recv, enb_recv, row_vg, col_vg, tri_vg, yrow, rowqk, triqk, m1, msend, mrecv, mcols, mdone, mback,
+def block_kernel(m_any, z_ref, mask_ref, res_ref, row_in_any, w_row_bias, row_out_any, col_in_any, col_out_any,
+                 w_opm_in, opm_out_any, start_in_any, w_start_bias, start_out_any, end_in_any, w_end_bias, end_out_any,
+                 mback, z_out,
+                 m_ref, w_row_in, w_row_out, w_col_in, w_col_out, w_opm_out, w_start_in, w_start_out, w_end_in, w_end_out,
+                 perm, perm_out, comp, compz, hperm, keep_row, mask_t, mask_s, norm, res_keep, wbt, bcol, bias,
+                 rowb_recv, stb_recv, enb_recv, row_vg, col_vg, tri_vg, yrow, rowqk, triqk, m1, msend, mrecv, mcols, mdone,
                  ycol, colqk,
                  left, crecv, cbig, outer, w2, w2t, ynorm, z1, zs, zr, z2, z3, zs2, zr2,
-                 send_sem, recv_sem, local_sem, c_send, c_recv, c_pair):
+                 send_sem, recv_sem, local_sem, load_sem, c_send, c_recv, c_pair):
     data = lax.axis_index('data')
     me = lax.axis_index('chip') * 4 + lax.axis_index('dap')
     core, chip_x, chip_y = lax.rem(me, 2), lax.rem(me // 2, 2), me // 4
@@ -194,12 +196,20 @@
     for r in range(1, NDEV):
         pl.semaphore_signal(barrier, inc=1, device_id=device(peer(r)), device_id_type=MESH)
 
+    loads = [pltpu.make_async_copy(src, dst, load_sem.at[n]) for n, (src, dst) in enumerate((
+        (row_in_any, w_row_in), (m_any, m_ref), (row_out_any, w_row_out), (col_in_any, w_col_in), (opm_out_any, w_opm_out),
+        (start_in_any, w_start_in), (end_in_any, w_end_in), (col_out_any, w_col_out), (start_out_any, w_start_out),
+        (end_out_any, w_end_out)))]
+    for load in loads:
+        load.start()
+
     r0, c0 = iota((256, 256), 0), iota((256, 256), 1)
     perm[...] = jnp.where(((r0 >> 4) == (c0 & 15)) & ((r0 & 15) == (c0 >> 4)), 1.0, 0.0).astype(BF16)
     perm_out[...] = jnp.where(((r0 >> 3) == (c0 & 31)) & ((r0 & 7) == (c0 >> 5)), 1.0, 0.0).astype(BF16)
-    perm_in[...] = jnp.where(((r0 >> 5) == (c0 & 7)) & ((r0 & 31) == (c0 >> 3)), 1.0, 0.0).astype(BF16)
     r1, c1 = iota((RES, LANES), 0), iota((RES, LANES), 1)
     comp[...] = jnp.where(((c1 & 15) < RLOC) & (r1 == (c1 >> 4) * RLOC + (c1 & 15)), 1.0, 0.0).astype(BF16)
+    compz[...] = jnp.where(((c1 & 7) < ZGROUP) & (r1 == ((c1 >> 3) & 7) * RLOC + (c1 >> 6) * ZGROUP + (c1 & 7)),
+                           1.0, 0.0).astype(BF16)
     r2, c2 = iota((LANES, LANES), 0), iota((LANES, LANES), 1)
     hperm[...] = jnp.where(((r2 >> 4) == (c2 & 7)) & ((r2 & 15) == (c2 >> 3)), 1.0, 0.0).astype(BF16)
     eye = jnp.where(r2 == c2, 1.0, 0.0).astype(BF16)
@@ -250,6 +260,8 @@
         pick = jnp.where(iota((SEQ, LANES), 0) == me * SLOC + i, 1.0, 0.0).astype(BF16)
         keep_row[i] = dot(mask_ref[...].astype(F32).astype(BF16), pick)
 
+    for load in loads:
+        load.wait()
     row_vg[...] = jnp.transpose(w_row_in[:, 2 * CM:])
     col_vg[...] = jnp.transpose(w_col_in[:, 2 * CM:])
     tri_vg[0] = jnp.transpose(w_start_in[:, 2 * CZ:])
@@ -267,7 +279,7 @@
     rowqk[:, :, RES:, :] = jnp.zeros((4, 4, LANES - RES, LANES), BF16)
     triqk[:, :, RES:, :] = jnp.zeros((2, RLOC, LANES - RES, LANES), BF16)
     z1[RLOC:, :, :] = jnp.zeros((16 - RLOC, RES, CZ), BF16)
-    z3[RLOC:, :, :] = jnp.zeros((16 - RLOC, RES, CZ), BF16)
+    z3[...] = jnp.zeros_like(z3)
 
     take_bias(rowb_recv, HM, ROWB)
 
@@ -376,7 +388,8 @@
 
     for j in range(RLOC - LAG, RLOC):
         relay(j)
-    mback[pl.ds(me * RLOC, RLOC)] = mdone[me]
+    keep_mine = local_copy(mdone.at[me], mback.at[pl.ds(me * RLOC, RLOC)], NCHUNK + 4)
+    keep_mine.start()
 
     def c_rows(s):
         return crecv.at[pl.ds(s * RLOC, RLOC)]
@@ -405,7 +418,13 @@
         update = update / (1e-3 + norm[pl.ds(me * RLOC + i, 1), :])
         z1[i] = add_residual(z_ref[i], jnp.transpose(update)[0:RES])
 
-    def triangle(state, result, w_in, which, w_out, recv, stage, late):
+    def z_src(buf, group):
+        return lambda d: buf.at[group, pl.ds(d * RLOC, RLOC)]
+
+    def z_dst(buf, group):
+        return lambda s: buf.at[group, s]
+
+    def triangle(state, result, w_in, which, w_out, recv, stage, late, send, zrecv, moved, zstage, slot):
         @pl.loop(0, RLOC)
         def _(i):
             ynorm[i, 0:RES, :] = layer_norm(state[i])
@@ -421,48 +440,34 @@
         for j in late:
             mb_start(j)
 
-        @pl.loop(0, RLOC // 4)
-        def _(blk):
+        for group in range(2):
+            first = group * ZGROUP
+
             def store(u, update):
-                result[blk * 4 + u] = add_residual(state[blk * 4 + u], update[0:RES])
-            attend_biased(range(4), 1, lambda u, t: triqk[0, blk * 4 + u], lambda u, t: triqk[1, blk * 4 + u, 0:RES],
-                          lambda u: dot_t(tri_vg[which - 1], ynorm[blk * 4 + u]).astype(BF16), bias,
+                result[u] = add_residual(state[u], update[0:RES])
+            attend_biased(range(first, first + ZGROUP), 1, lambda u, t: triqk[0, u], lambda u, t: triqk[1, u, 0:RES],
+                          lambda u: dot_t(tri_vg[which - 1], ynorm[u]).astype(BF16), bias,
                           lambda u: res_keep[...], w_out[...], store)
-
-    def z_src(buf):
-        return lambda d: buf.at[pl.ds(d * RLOC, RLOC)]
-
-    def z_dst(buf):
-        return lambda s: buf.at[s]
-
-    def exchange(state, send, recv, result, stage, n):
-        for j in range(RES // 16):
-            blk = state[:, 16 * j:16 * j + 16, :].reshape(256, CZ)
-            send[16 * j:16 * j + 16] = dot(perm[...], blk).astype(BF16).reshape(16, 16, CZ)
-        start_all(stage, z_src(send), z_dst(recv))
-        own = local_copy(z_src(send)(me), z_dst(recv)(me), n)
-        own.start()
-        own.wait()
-        wait_recv(stage, z_dst(recv))
+            for j in range(RES // 32):
+                blk = result[first:first + 8, 32 * j:32 * j + 32, :].reshape(256, CZ)
+                send[group, 32 * j:32 * j + 32] = dot(perm_out[...], blk).reshape(32, 8, CZ).astype(BF16)
+            start_all(zstage + group, z_src(send, group), z_dst(zrecv, group))
+            local_copy(z_src(send, group)(me), z_dst(zrecv, group)(me), slot + group).start()
+
+        for group in range(2):
+            local_copy(z_src(send, group)(me), z_dst(zrecv, group)(me), slot + group).wait()
+            wait_recv(zstage + group, z_dst(zrecv, group))
 
         @pl.loop(0, RLOC)
         def _(i):
-            result[i] = dot(comp[...], recv[:, i].reshape(LANES, CZ)).astype(BF16)
-
-    triangle(z1, z1, w_start_in, 1, w_start_out, stb_recv, STB, (MB_EARLY + 3, MB_EARLY + 4))
-    exchange(z1, zs, zr, z2, ZF, NCHUNK)
-    triangle(z2, z3, w_end_in, 2, w_end_out, enb_recv, ENB, (MB_EARLY + 5,))
-    exchange(z3, zs2, zr2, z_out, ZB, NCHUNK + 1)
-
-    def mb_dst(s):
-        return mback.at[pl.ds(s * RLOC, RLOC)]
-    wait_recv(MB, mb_dst)
-    for q in range(NCHUNK):
-        @pl.loop(0, RES // 32)
-        def _(j):
-            blk = mback[pl.ds(j * 32, 32), q].astype(F32).reshape(256, CM).astype(BF16)
-            rows = dot(perm_in[...], blk).astype(BF16).reshape(CHUNK, 32, CM)
-            m_out[CHUNK * q:CHUNK * q + CHUNK, pl.ds(pl.multiple_of(j * 32, 32), 32), :] = rows
+            rows = zrecv[:, :, i].astype(F32).reshape(LANES, CZ).astype(BF16)
+            moved[i] = dot(compz[...], rows).astype(BF16)
+
+    triangle(z1, z1, w_start_in, 1, w_start_out, stb_recv, STB, (MB_EARLY + 3,), zs, zr, z2, ZF, NCHUNK)
+    triangle(z2, z3, w_end_in, 2, w_end_out, enb_recv, ENB, (), zs2, zr2, z_out, ZB, NCHUNK + 2)
+
+    wait_recv(MB, lambda s: mback.at[pl.ds(s * RLOC, RLOC)])
+    keep_mine.wait()
 
     wait_send(ROWB, lambda d: bias_rows(rowb_recv)(me))
     for q in range(NCHUNK):
@@ -472,22 +477,26 @@
         rows = c_rows(me if t in (0, 1, 2, 6) else twins[t - 3])
         remote(rows, rows, c_send.at[t], c_pair.at[0], partner).wait_send()
     wait_send(STB, lambda d: bias_rows(stb_recv)(me))
-    wait_send(ZF, z_src(zs))
+    for group in range(2):
+        wait_send(ZF + group, z_src(zs, group))
     wait_send(ENB, lambda d: bias_rows(enb_recv)(me))
-    wait_send(ZB, z_src(zs2))
+    for group in range(2):
+        wait_send(ZB + group, z_src(zs2, group))
 
 
 def solution(mesh):
     rows = P(('data', 'chip', 'dap'))
     in_specs = (rows, rows, P('data'), P('data')) + (P(),) * 13
     vmem = pl.BlockSpec(memory_space=pltpu.VMEM)
+    hbm = pl.BlockSpec(memory_space=pl.ANY)
 
     def per_device(m_blk, z_blk, msa_mask, res_mask, w_row_in, w_row_bias, w_row_out, w_col_in, w_col_out,
                    w_opm_in, w_opm_out, w_start_in, w_start_bias, w_start_out, w_end_in, w_end_bias, w_end_out):
-        scratch = [
+        loaded = [m_blk, w_row_in, w_row_out, w_col_in, w_col_out, w_opm_out, w_start_in, w_start_out, w_end_in, w_end_out]
+        scratch = [pltpu.VMEM(x.shape, x.dtype) for x in loaded] + [
             pltpu.VMEM((256, 256), BF16),
             pltpu.VMEM((256, 256), BF16),
-            pltpu.VMEM((256, 256), BF16),
+            pltpu.VMEM((RES, LANES), BF16),
             pltpu.VMEM((RES, LANES), BF16),
             pltpu.VMEM((LANES, LANES), BF16),
             pltpu.VMEM((SLOC, RES, LANES), F32),
@@ -512,7 +521,6 @@
             pltpu.VMEM((NCHUNK, NDEV, RLOC, CHUNK, CM), BF16),
             pltpu.VMEM((NCHUNK, RLOC, CROWS, CM), BF16),
             pltpu.VMEM((NDEV, RLOC, NCHUNK, CHUNK, CM), BF16),
-            pltpu.VMEM((RES, NCHUNK, CHUNK, CM), BF16),
             pltpu.VMEM((RLOC, SEQ, CM), BF16),
             pltpu.VMEM((4, RLOC, SEQ, LANES), BF16),
             pltpu.VMEM((RLOC, OPM, SEQ), BF16),
@@ -523,29 +531,31 @@
             pltpu.VMEM((CZ, OPM * OPM), BF16),
             pltpu.VMEM((RLOC, LANES, CZ), BF16),
             pltpu.VMEM((16, RES, CZ), BF16),
-            pltpu.VMEM((RES, 16, CZ), BF16),
-            pltpu.VMEM((NDEV, RLOC, 16, CZ), BF16),
+            pltpu.VMEM((2, RES, 8, CZ), BF16),
+            pltpu.VMEM((2, NDEV, RLOC, 8, CZ), BF16),
             pltpu.VMEM((RLOC, RES, CZ), BF16),
             pltpu.VMEM((16, RES, CZ), BF16),
-            pltpu.VMEM((RES, 16, CZ), BF16),
-            pltpu.VMEM((NDEV, RLOC, 16, CZ), BF16),
+            pltpu.VMEM((2, RES, 8, CZ), BF16),
+            pltpu.VMEM((2, NDEV, RLOC, 8, CZ), BF16),
             pltpu.SemaphoreType.DMA((NSTAGE, NDEV)),
             pltpu.SemaphoreType.DMA((NSTAGE, NDEV)),
-            pltpu.SemaphoreType.DMA((NCHUNK + 2,)),
+            pltpu.SemaphoreType.DMA((NCHUNK + 5,)),
+            pltpu.SemaphoreType.DMA((10,)),
             pltpu.SemaphoreType.DMA((7,)),
             pltpu.SemaphoreType.DMA((3, RLOC)),
             pltpu.SemaphoreType.DMA((4,)),
         ]
-        return pl.pallas_call(
+        m_home, z_new = pl.pallas_call(
             block_kernel,
             name='evoformer_block',
-            out_shape=(jax.ShapeDtypeStruct(m_blk.shape, BF16), jax.ShapeDtypeStruct(z_blk.shape, BF16)),
-            in_specs=[vmem] * 17,
-            out_specs=(vmem, vmem),
+            out_shape=(jax.ShapeDtypeStruct((RES, NCHUNK, CHUNK, CM), BF16), jax.ShapeDtypeStruct(z_blk.shape, BF16)),
+            in_specs=[hbm, vmem, vmem, vmem, hbm, vmem, hbm, hbm, hbm, vmem, hbm, hbm, vmem, hbm, hbm, vmem, hbm],
+            out_specs=(hbm, vmem),
             scratch_shapes=scratch,
             compiler_params=pltpu.CompilerParams(collective_id=0, has_side_effects=True,
                                                  vmem_limit_bytes=56 * 1024 * 1024),
         )(m_blk, z_blk, msa_mask.T, res_mask.reshape(1, RES), w_row_in, w_row_bias.T, w_row_out, w_col_in, w_col_out,
           w_opm_in.T, w_opm_out, w_start_in, w_start_bias.T, w_start_out, w_end_in, w_end_bias.T, w_end_out)
+        return jnp.swapaxes(m_home.reshape(RES, SLOC, CM), 0, 1), z_new
 
     return jax.shard_map(per_device, mesh=mesh, in_specs=in_specs, out_specs=(rows, rows), check_vma=False)

time: 123 us -> 117 us (0.951)
  Pallas kernels: 119 us -> 112 us
    pallas_call x1, Pallas kernels: 119 us -> 112 us  [per_device(): pl.pallas_call(block_kernel, name='evoformer_block', out_shape=(jax.Shape...]
    reshape x0 -> x1, local copies, waits for them, and re-layouts: none -> 3.47 us  [per_device(): return (jnp.swapaxes(m_home.reshape(RES, SLOC, CM), 0, 1), z_new)]
    unnamed x4 -> x3, local copies, waits for them, and re-layouts: 3.41 us -> 0.72 us
where the time goes in v5:
time: 117 us
  Pallas kernels  112 us (96%)
  local copies, waits for them, and re-layouts  4.19 us (4%)
    pallas_call x1, Pallas kernels, per_device(): pl.pallas_call(block_kernel, name='evoformer_block', out_shape=(jax.Shape...  112 us
    reshape x1, local copies, waits for them, and re-layouts, per_device(): return (jnp.swapaxes(m_home.reshape(RES, SLOC, CM), 0, 1), z_new)  3.47 us

profile of v5, /device:TPU:0, one launch (start us, length us, event | category | flops | bytes accessed | tf_op | source)
XLA Modules:
  0.0 117.3 jit_solution(6387495613415330618)
XLA Ops:
  0.6 112.4 %evoformer_block.1 = (bf16[96,4,8,256]{3,2,1,0:T(8,128)(2,1)}, bf16[12,96,128]{2,1,0:T(8,128)(2,1)}) custom-call(bf16[32,96,256]{2,1,0:T(8,128)(2,1)} %m_any.1, bf16[12,96,128]{2,1,0:T(8,128)(2,1)} %z_ref.1, s32[96,256]{1,0:T(8,128)} %bitcast.12, s32[1,96]{1,0:T(1,128)} %bitcast.17, bf16[256,1024]{1,0:T(8,128)(2,1)} %row_in_any.1, bf16[8,128]{1,0:T(8,128)(2,1)} %bitcast.14, ...), custom_call_target="tpu_custom_call" | custom-call | tf_op jit(solution)/shard_map/evoformer_block/pallas_call | solution.py:548
  113.1 0.0 copy-start
  113.1 3.5 %copy.21 = bf16[96,32,256]{2,0,1:T(8,128)(2,1)} copy(bf16[96,32,256]{2,1,0:T(8,128)(2,1)} %bitcast.11) | data formatting | bytes 3145728 | tf_op jit(solution)/shard_map/reshape | solution.py:559
  116.6 0.0 copy-done
  116.6 0.7 copy.23
Async XLA Ops:
  113.1 3.5 %copy-start = (bf16[12,96,128]{2,1,0:T(8,128)(2,1)S(1)}, bf16[12,96,128]{2,1,0:T(8,128)(2,1)}, u32[]{:S(2)}) copy-start(bf16[12,96,128]{2,1,0:T(8,128)(2,1)} %get-tuple-element.9) | copy-start | bytes 884740

commit v6 on v5

--- a/solution.py
+++ b/solution.py
@@ -2,6 +2,7 @@
 
 import jax
 import jax.numpy as jnp
+import numpy as np
 from jax import lax
 from jax.experimental import pallas as pl
 from jax.experimental.pallas import tpu as pltpu
@@ -17,7 +18,16 @@
 LANES = 128
 MASKED = -1e9
 SCALE = HD ** -0.5
-LOG2E = 1.4426950408889634
+
+
+def bf16_parts(value, n):
+    parts = []
+    for _ in range(n):
+        parts.append(float(np.asarray(value - sum(parts), np.float32).astype(BF16)))
+    return parts
+
+
+MASKED_SCORE = bf16_parts(MASKED / SCALE, 3)
 
 ROWB, MF, MB, STB, ZF, ENB, ZB = 0, 1, 5, 6, 7, 9, 10
 NSTAGE = 12
@@ -25,7 +35,7 @@
 CHUNK = 8
 NCHUNK = SLOC // CHUNK
 CROWS = NDEV * CHUNK
-LAG = 2
+LAG = 4
 MB_EARLY = 8
 
 
@@ -65,28 +75,28 @@
     return lax.dot_general(a, b, (((0,), (0,)), ((), ())), preferred_element_type=F32)
 
 
-def softmax_keys(logits, exponential=jnp.exp):
-    weights = exponential(logits - jnp.max(logits, axis=0, keepdims=True))
+def softmax_keys(logits):
+    weights = jnp.exp(logits - jnp.max(logits, axis=0, keepdims=True))
     return (weights * (1.0 / jnp.sum(weights, axis=0, keepdims=True))).astype(BF16)
 
 
-def pipeline(items, first, middle, last, finish):
-    opened, ready = {0: first(items[0])}, {}
-    for n in range(len(items) + 2):
-        if n + 1 < len(items):
-            opened[n + 1] = first(items[n + 1])
-        if n < len(items):
+def pipeline(items, first, middle, last, finish, ahead=1, behind=1):
+    count = len(items)
+    opened, ready = {}, {}
+    for n in range(-ahead, count + behind + 1):
+        if n + ahead < count:
+            opened[n + ahead] = first(items[n + ahead])
+        if 0 <= n < count:
             ready[n] = middle(items[n], opened.pop(n))
-        if 1 <= n <= len(items):
-            last(items[n - 1], ready.pop(n - 1))
-        if n >= 2:
-            finish(items[n - 2])
+        if 0 <= n - behind < count:
+            last(items[n - behind], ready.pop(n - behind))
+        if 0 <= n - behind - 1 < count:
+            finish(items[n - behind - 1])
 
 
 def attend_biased(rows, tiles, q_of, k_of, vg_of, bias_ref, keep_of, w_out, store):
     masks = head_masks()
     each = len(masks)
-    offsets = {u: (keep_of(u) - 1.0) * -MASKED for u in rows}
     vgs = {}
     mixed = {u: [] for u in rows}
 
@@ -99,7 +109,8 @@
 
     def middle(item, scores):
         u, t = item
-        return [softmax_keys((scores[n * RES:(n + 1) * RES] * SCALE + bias_ref[each * t + n]) * keep_of(u) + offsets[u])
+        keep = keep_of(u) != 0.0
+        return [softmax_keys(jnp.where(keep, scores[n * RES:(n + 1) * RES] * SCALE + bias_ref[each * t + n], MASKED))
                 for n in range(each)]
 
     def last(item, probs):
@@ -118,34 +129,37 @@
     pipeline([(u, t) for u in rows for t in range(tiles)], first, middle, last, finish)
 
 
-def attend_column(residues, q_of, k_of, vg_of, keep_of, w_out, store):
+def attend_column(residues, q_of, k_of, aug_of, ones, vg_of, w_out, store):
     masks = head_masks()
     each = len(masks)
-    keeps, vgs = {}, {}
-    mixed = {u: [] for u in residues}
+    halves = SEQ // LANES
+    vgs, keys = {}, {}
+    mixed = {(u, half): [] for u in residues for half in range(halves)}
 
     def first(item):
-        u, h = item
-        if h == 0:
-            keeps[u] = keep_of(u)
+        u, h, half = item
+        if (h, half) == (0, 0):
             vgs[u] = vg_of(u)
-        return dot_t(only_head(k_of(u, h // each), masks[h % each]), q_of(u, h // each))
+        if half == 0:
+            keys[u, h] = jnp.concatenate([only_head(k_of(u, h // each), masks[h % each]), aug_of(u)], axis=1)
+        q = q_of(u, h // each)[half * LANES:(half + 1) * LANES]
+        return dot_t(keys[u, h], jnp.concatenate([q, ones], axis=1))
 
     def middle(item, scores):
-        keep = keeps[item[0]]
-        return softmax_keys(scores * (keep * (SCALE * LOG2E)) + (keep - 1.0) * (-MASKED * LOG2E), jnp.exp2)
+        return softmax_keys(scores * SCALE)
 
     def last(item, probs):
-        u, h = item
-        mixed[u].append(dot(vgs[u][h * HD:(h + 1) * HD], probs))
+        u, h, half = item
+        mixed[u, half].append(dot(vgs[u][h * HD:(h + 1) * HD], probs))
 
     def finish(item):
-        u, h = item
-        if h == HM - 1:
+        u, h, half = item
+        if (h, half) == (HM - 1, halves - 1):
             gates = jax.nn.sigmoid(vgs[u][CM:].astype(F32))
-            store(u, dot_tl((jnp.concatenate(mixed[u], axis=0) * gates).astype(BF16), w_out))
-
-    pipeline([(u, h) for u in residues for h in range(HM)], first, middle, last, finish)
+            out = jnp.concatenate([jnp.concatenate(mixed[u, n], axis=0) for n in range(halves)], axis=1)
+            store(u, dot_tl((out * gates).astype(BF16), w_out))
+
+    pipeline([(u, h, half) for u in residues for h in range(HM) for half in range(halves)], first, middle, last, finish, 4, 2)
 
 
 def block_kernel(m_any, z_ref, mask_ref, res_ref, row_in_any, w_row_bias, row_out_any, col_in_any, col_out_any,
@@ -154,7 +168,7 @@
                  m_ref, w_row_in, w_row_out, w_col_in, w_col_out, w_opm_out, w_start_in, w_start_out, w_end_in, w_end_out,
                  perm, perm_out, comp, compz, hperm, keep_row, mask_t, mask_s, norm, res_keep, wbt, bcol, bias,
                  rowb_recv, stb_recv, enb_recv, row_vg, col_vg, tri_vg, yrow, rowqk, triqk, m1, msend, mrecv, mcols, mdone,
-                 ycol, colqk,
+                 ycol, colqk, caug, ckeep, ones,
                  left, crecv, cbig, outer, w2, w2t, ynorm, z1, zs, zr, z2, z3, zs2, zr2,
                  send_sem, recv_sem, local_sem, load_sem, c_send, c_recv, c_pair):
     data = lax.axis_index('data')
@@ -213,6 +227,7 @@
     r2, c2 = iota((LANES, LANES), 0), iota((LANES, LANES), 1)
     hperm[...] = jnp.where(((r2 >> 4) == (c2 & 7)) & ((r2 & 15) == (c2 >> 3)), 1.0, 0.0).astype(BF16)
     eye = jnp.where(r2 == c2, 1.0, 0.0).astype(BF16)
+    ones[...] = jnp.where(iota((SEQ, LANES), 1) < len(MASKED_SCORE), 1.0, 0.0).astype(BF16)
     bcol[...] = jnp.zeros_like(bcol)
     wbt[...] = jnp.zeros_like(wbt)
     for n, w in enumerate((w_row_bias, w_start_bias, w_end_bias)):
@@ -351,10 +366,17 @@
 
     @pl.loop(0, RLOC // 2)
     def _(pair):
-        def keep_of(u):
+        lane = iota((SEQ, LANES), 1)
+        offset = jnp.zeros((SEQ, LANES), F32)
+        for n, part in enumerate(MASKED_SCORE):
+            offset = jnp.where(lane == n, part, offset)
+        for u in range(2):
             pick = jnp.where(iota((RES, LANES), 0) == me * RLOC + pair * 2 + u, 1.0, 0.0).astype(BF16)
             keep = dot(mask_s[...], pick)
-            return jnp.concatenate([keep, keep], axis=1)
+            caug[u] = ((1.0 - keep) * offset).astype(BF16)
+            keep = keep.astype(BF16)
+            for t in range(2):
+                ckeep[u, t] = colqk[2 + t, pair * 2 + u] * keep
 
         def store(u, update):
             j = pair * 2 + u
@@ -367,8 +389,8 @@
             for d in range(NDEV):
                 mdone[d, j] = done[:, d]
 
-        attend_column(range(2), lambda u, t: colqk[t, pair * 2 + u], lambda u, t: colqk[2 + t, pair * 2 + u],
-                      lambda u: dot_t(col_vg[...], ycol[pair * 2 + u]).astype(BF16), keep_of, w_col_out[...], store)
+        attend_column(range(2), lambda u, t: colqk[t, pair * 2 + u], lambda u, t: ckeep[u, t], lambda u: caug[u],
+                      ones[0:LANES], lambda u: dot_t(col_vg[...], ycol[pair * 2 + u]).astype(BF16), w_col_out[...], store)
         for u in range(2):
             j = pair * 2 + u
             row = crecv.at[me * RLOC + j]
@@ -376,10 +398,10 @@
                 remote(row, row, c_send.at[t], c_recv.at[t, j], twin).start()
             remote(row, row, c_send.at[6], c_pair.at[3], partner).start()
 
-        @pl.when(pair >= 1)
+        @pl.when(pair >= LAG // 2)
         def _():
             for u in range(2):
-                relay(pair * 2 - 2 + u)
+                relay(pair * 2 - LAG + u)
 
         @pl.when(pair < MB_EARLY // 2)
         def _():
@@ -523,6 +545,9 @@
             pltpu.VMEM((NDEV, RLOC, NCHUNK, CHUNK, CM), BF16),
             pltpu.VMEM((RLOC, SEQ, CM), BF16),
             pltpu.VMEM((4, RLOC, SEQ, LANES), BF16),
+            pltpu.VMEM((2, SEQ, LANES), BF16),
+            pltpu.VMEM((2, 2, SEQ, LANES), BF16),
+            pltpu.VMEM((SEQ, LANES), BF16),
             pltpu.VMEM((RLOC, OPM, SEQ), BF16),
             pltpu.VMEM((RES, OPM, SEQ), BF16),
             pltpu.VMEM((OPM, LANES, SEQ), BF16),

time: 117 us -> 117 us (level)
  no operation moved by 1% of the time
where the time goes in v6:
time: 117 us; the launch traced here: 116 us
  Pallas kernels  112 us (96%)
  local copies, waits for them, and re-layouts  4.19 us (4%)
    pallas_call x1, Pallas kernels, per_device(): pl.pallas_call(block_kernel, name='evoformer_block', out_shape=(jax.Shape...  112 us
    reshape x1, local copies, waits for them, and re-layouts, per_device(): return (jnp.swapaxes(m_home.reshape(RES, SLOC, CM), 0, 1), z_new)  3.47 us

profile of v6, /device:TPU:0, one launch (start us, length us, event | category | flops | bytes accessed | tf_op | source)
XLA Modules:
  0.0 116.4 jit_solution(7356034873390861674)
XLA Ops:
  0.6 111.6 %evoformer_block.1 = (bf16[96,4,8,256]{3,2,1,0:T(8,128)(2,1)}, bf16[12,96,128]{2,1,0:T(8,128)(2,1)}) custom-call(bf16[32,96,256]{2,1,0:T(8,128)(2,1)} %m_any.1, bf16[12,96,128]{2,1,0:T(8,128)(2,1)} %z_ref.1, s32[96,256]{1,0:T(8,128)} %bitcast.12, s32[1,96]{1,0:T(1,128)} %bitcast.17, bf16[256,1024]{1,0:T(8,128)(2,1)} %row_in_any.1, bf16[8,128]{1,0:T(8,128)(2,1)} %bitcast.14, ...), custom_call_target="tpu_custom_call" | custom-call | tf_op jit(solution)/shard_map/evoformer_block/pallas_call | solution.py:573
  112.2 0.0 copy-start
  112.2 3.5 %copy.21 = bf16[96,32,256]{2,0,1:T(8,128)(2,1)} copy(bf16[96,32,256]{2,1,0:T(8,128)(2,1)} %bitcast.11) | data formatting | bytes 3145728 | tf_op jit(solution)/shard_map/reshape | solution.py:584
  115.7 0.0 copy-done
  115.7 0.7 copy.23
Async XLA Ops:
  112.2 3.5 %copy-start = (bf16[12,96,128]{2,1,0:T(8,128)(2,1)S(1)}, bf16[12,96,128]{2,1,0:T(8,128)(2,1)}, u32[]{:S(2)}) copy-start(bf16[12,96,128]{2,1,0:T(8,128)(2,1)} %get-tuple-element.9) | copy-start | bytes 884740

commit v7 on v6

--- a/solution.py
+++ b/solution.py
@@ -37,6 +37,7 @@
 CROWS = NDEV * CHUNK
 LAG = 4
 MB_EARLY = 8
+NRES = 2
 
 
 def dot(a, b):
@@ -364,22 +365,22 @@
             remote(row, row, c_send.at[t], c_recv.at[t, j], twin).wait_recv()
             remote(row, row, c_send.at[3 + t], c_pair.at[t], partner).start()
 
-    @pl.loop(0, RLOC // 2)
+    @pl.loop(0, RLOC // NRES)
     def _(pair):
         lane = iota((SEQ, LANES), 1)
         offset = jnp.zeros((SEQ, LANES), F32)
         for n, part in enumerate(MASKED_SCORE):
             offset = jnp.where(lane == n, part, offset)
-        for u in range(2):
-            pick = jnp.where(iota((RES, LANES), 0) == me * RLOC + pair * 2 + u, 1.0, 0.0).astype(BF16)
+        for u in range(NRES):
+            pick = jnp.where(iota((RES, LANES), 0) == me * RLOC + pair * NRES + u, 1.0, 0.0).astype(BF16)
             keep = dot(mask_s[...], pick)
             caug[u] = ((1.0 - keep) * offset).astype(BF16)
             keep = keep.astype(BF16)
             for t in range(2):
-                ckeep[u, t] = colqk[2 + t, pair * 2 + u] * keep
+                ckeep[u, t] = colqk[2 + t, pair * NRES + u] * keep
 
         def store(u, update):
-            j = pair * 2 + u
+            j = pair * NRES + u
             mask_row = mask_t[pl.ds(me * RLOC + j, 1), :]
             x = add_residual(mcols[:, j].reshape(SEQ, CM), update)
             both = dot_t(w_opm_in[...], layer_norm(x)).astype(BF16).astype(F32) * mask_row
@@ -389,24 +390,24 @@
             for d in range(NDEV):
                 mdone[d, j] = done[:, d]
 
-        attend_column(range(2), lambda u, t: colqk[t, pair * 2 + u], lambda u, t: ckeep[u, t], lambda u: caug[u],
-                      ones[0:LANES], lambda u: dot_t(col_vg[...], ycol[pair * 2 + u]).astype(BF16), w_col_out[...], store)
-        for u in range(2):
-            j = pair * 2 + u
+        attend_column(range(NRES), lambda u, t: colqk[t, pair * NRES + u], lambda u, t: ckeep[u, t], lambda u: caug[u],
+                      ones[0:LANES], lambda u: dot_t(col_vg[...], ycol[pair * NRES + u]).astype(BF16), w_col_out[...], store)
+        for u in range(NRES):
+            j = pair * NRES + u
             row = crecv.at[me * RLOC + j]
             for t, twin in enumerate(twins):
                 remote(row, row, c_send.at[t], c_recv.at[t, j], twin).start()
             remote(row, row, c_send.at[6], c_pair.at[3], partner).start()
 
-        @pl.when(pair >= LAG // 2)
+        @pl.when(pair >= LAG // NRES)
         def _():
-            for u in range(2):
-                relay(pair * 2 - LAG + u)
-
-        @pl.when(pair < MB_EARLY // 2)
+            for u in range(NRES):
+                relay(pair * NRES - LAG + u)
+
+        @pl.when(pair < MB_EARLY // NRES)
         def _():
-            for u in range(2):
-                mb_start(pair * 2 + u)
+            for u in range(NRES):
+                mb_start(pair * NRES + u)
 
     for j in range(RLOC - LAG, RLOC):
         relay(j)
@@ -504,6 +505,18 @@
     wait_send(ENB, lambda d: bias_rows(enb_recv)(me))
     for group in range(2):
         wait_send(ZB + group, z_src(zs2, group))
+
+
+def finish_kernel(m_home, z_new, m_out, z_out, perm_in):
+    @pl.when(pl.program_id(0) == 0)
+    def _():
+        r, c = iota((256, 256), 0), iota((256, 256), 1)
+        perm_in[...] = jnp.where(((r >> 5) == (c & 7)) & ((r & 31) == (c >> 3)), 1.0, 0.0).astype(BF16)
+        z_out[...] = z_new[...]
+
+    for j in range(RES // 32):
+        blk = m_home[32 * j:32 * j + 32, 0].astype(F32).reshape(256, CM).astype(BF16)
+        m_out[:, 32 * j:32 * j + 32, :] = dot(perm_in[...], blk).astype(BF16).reshape(CHUNK, 32, CM)
 
 
 def solution(mesh):
@@ -545,8 +558,8 @@
             pltpu.VMEM((NDEV, RLOC, NCHUNK, CHUNK, CM), BF16),
             pltpu.VMEM((RLOC, SEQ, CM), BF16),
             pltpu.VMEM((4, RLOC, SEQ, LANES), BF16),
-            pltpu.VMEM((2, SEQ, LANES), BF16),
-            pltpu.VMEM((2, 2, SEQ, LANES), BF16),
+            pltpu.VMEM((NRES, SEQ, LANES), BF16),
+            pltpu.VMEM((NRES, 2, SEQ, LANES), BF16),
             pltpu.VMEM((SEQ, LANES), BF16),
             pltpu.VMEM((RLOC, OPM, SEQ), BF16),
             pltpu.VMEM((RES, OPM, SEQ), BF16),
@@ -581,6 +594,16 @@
                                                  vmem_limit_bytes=56 * 1024 * 1024),
         )(m_blk, z_blk, msa_mask.T, res_mask.reshape(1, RES), w_row_in, w_row_bias.T, w_row_out, w_col_in, w_col_out,
           w_opm_in.T, w_opm_out, w_start_in, w_start_bias.T, w_start_out, w_end_in, w_end_bias.T, w_end_out)
-        return jnp.swapaxes(m_home.reshape(RES, SLOC, CM), 0, 1), z_new
+        whole = pl.BlockSpec((RLOC, RES, CZ), lambda q: (0, 0, 0))
+        return pl.pallas_call(
+            finish_kernel,
+            name='finish',
+            grid=(NCHUNK,),
+            out_shape=(jax.ShapeDtypeStruct(m_blk.shape, BF16), jax.ShapeDtypeStruct(z_blk.shape, BF16)),
+            in_specs=[pl.BlockSpec((RES, 1, CHUNK, CM), lambda q: (0, q, 0, 0)), whole],
+            out_specs=(pl.BlockSpec((CHUNK, RES, CM), lambda q: (q, 0, 0)), whole),
+            scratch_shapes=[pltpu.VMEM((256, 256), BF16)],
+            compiler_params=pltpu.CompilerParams(dimension_semantics=('arbitrary',)),
+        )(m_home, z_new)
 
     return jax.shard_map(per_device, mesh=mesh, in_specs=in_specs, out_specs=(rows, rows), check_vma=False)

time: 117 us -> 117 us (level)
  local copies, waits for them, and re-layouts: 4.19 us -> 0 us
  Pallas kernels: 112 us -> 116 us
    pallas_call x0 -> x1, Pallas kernels: none -> 4.22 us  [per_device(): pl.pallas_call(finish_kernel, name='finish', grid=(NCHUNK,), out_shape=(j...]
    reshape x1 -> x0, local copies, waits for them, and re-layouts: 3.47 us -> none  [per_device(): return (jnp.swapaxes(m_home.reshape(RES, SLOC, CM), 0, 1), z_new)]
where the time goes in v7:
time: 117 us; the launch traced here: 116 us
  Pallas kernels  116 us (99%)
    pallas_call x1, Pallas kernels, per_device(): pl.pallas_call(block_kernel, name='evoformer_block', out_shape=(jax.Shape...  112 us
    pallas_call x1, Pallas kernels, per_device(): pl.pallas_call(finish_kernel, name='finish', grid=(NCHUNK,), out_shape=(j...  4.22 us

profile of v7, /device:TPU:0, one launch (start us, length us, event | category | flops | bytes accessed | tf_op | source)
XLA Modules:
  0.0 116.4 jit_solution(10202812313774097521)
XLA Ops:
  0.6 111.5 %evoformer_block.1 = (bf16[96,4,8,256]{3,2,1,0:T(8,128)(2,1)}, bf16[12,96,128]{2,1,0:T(8,128)(2,1)}) custom-call(bf16[32,96,256]{2,1,0:T(8,128)(2,1)} %m_any.1, bf16[12,96,128]{2,1,0:T(8,128)(2,1)} %z_ref.1, s32[96,256]{1,0:T(8,128)} %bitcast.6, s32[1,96]{1,0:T(1,128)} %bitcast.11, bf16[256,1024]{1,0:T(8,128)(2,1)} %row_in_any.1, bf16[8,128]{1,0:T(8,128)(2,1)} %bitcast.8, ...), custom_call_target="tpu_custom_call" | custom-call | tf_op jit(solution)/shard_map/evoformer_block/pallas_call | solution.py:586
  112.2 4.2 %finish.1 = (bf16[32,96,256]{2,1,0:T(8,128)(2,1)}, bf16[12,96,128]{2,1,0:T(8,128)(2,1)}) custom-call(bf16[96,4,8,256]{3,2,1,0:T(8,128)(2,1)} %get-tuple-element.4.m_home, bf16[12,96,128]{2,1,0:T(8,128)(2,1)} %get-tuple-element.5.z_new), custom_call_target="tpu_custom_call" | custom-call | tf_op jit(solution)/shard_map/finish/pallas_call | solution.py:598

commit v8 on v7

--- a/solution.py
+++ b/solution.py
@@ -36,7 +36,7 @@
 NCHUNK = SLOC // CHUNK
 CROWS = NDEV * CHUNK
 LAG = 4
-MB_EARLY = 8
+MB_EARLY = 10
 NRES = 2
 
 
@@ -237,8 +237,7 @@
     def send_bias(recv, which, heads, stage):
         weights = wbt[which].astype(BF16)
 
-        @pl.loop(0, RLOC)
-        def _(i):
+        for i in range(RLOC):
             bcol[i] = dot_t(weights, ynorm[i])
 
         mine = dot(hperm[0:heads * 16, :], bcol[...].reshape(LANES, LANES).astype(BF16)).astype(BF16)
@@ -256,9 +255,7 @@
 
     ynorm[:, RES:, :] = jnp.zeros((RLOC, LANES - RES, CZ), BF16)
 
-    @pl.loop(0, RLOC)
-    def _(i):
-        ynorm[i, 0:RES, :] = layer_norm(z_ref[i])
+    ynorm[:, 0:RES, :] = layer_norm(z_ref[...].reshape(RLOC * RES, CZ)).reshape(RLOC, RES, CZ)
 
     pl.semaphore_wait(barrier, NDEV - 1)
     send_bias(rowb_recv, 0, HM, ROWB)
@@ -271,10 +268,11 @@
     mask_t[...] = dot(mt, seq_order)
     mask_s[...] = dot_t(seq_rows, mt).astype(BF16)
 
-    @pl.loop(0, SLOC)
-    def _(i):
-        pick = jnp.where(iota((SEQ, LANES), 0) == me * SLOC + i, 1.0, 0.0).astype(BF16)
-        keep_row[i] = dot(mask_ref[...].astype(F32).astype(BF16), pick)
+    @pl.loop(0, SLOC // 4)
+    def _(blk):
+        for u in range(4):
+            pick = jnp.where(iota((SEQ, LANES), 0) == me * SLOC + blk * 4 + u, 1.0, 0.0).astype(BF16)
+            keep_row[blk * 4 + u] = dot(mask_ref[...].astype(F32).astype(BF16), pick)
 
     for load in loads:
         load.wait()
@@ -335,16 +333,15 @@
         local_copy(m_src(q)(me), m_dst(q)(me), q).wait()
         wait_recv(MF + q, m_dst(q))
 
-        @pl.loop(0, RLOC // 4)
-        def _(blk):
+        for blk in range(RLOC // 4):
             x = jnp.concatenate([mrecv[q, :, blk * 4 + u].astype(F32).reshape(CROWS, CM) for u in range(4)], axis=0)
             for u in range(4):
                 mcols[q, blk * 4 + u] = x[u * CROWS:(u + 1) * CROWS].astype(BF16)
             y = layer_norm(x)
-            ycol[pl.ds(blk * 4, 4), CROWS * q:CROWS * q + CROWS, :] = y.reshape(4, CROWS, CM)
+            ycol[blk * 4:blk * 4 + 4, CROWS * q:CROWS * q + CROWS, :] = y.reshape(4, CROWS, CM)
             qk = dot(y, w_col_in[:, 0:2 * CM]).astype(BF16)
             for t in range(4):
-                colqk[t, pl.ds(blk * 4, 4), CROWS * q:CROWS * q + CROWS, :] = (
+                colqk[t, blk * 4:blk * 4 + 4, CROWS * q:CROWS * q + CROWS, :] = (
                     qk[:, t * LANES:(t + 1) * LANES].reshape(4, CROWS, LANES))
 
     row_chunk(0)
@@ -420,26 +417,28 @@
     for t, first in enumerate(twins + (me,)):
         rows = c_rows(first + 1 - 2 * core)
         remote(rows, rows, c_send.at[3 + t], c_pair.at[t], partner).wait_recv()
-    for j in range(MB_EARLY, MB_EARLY + 3):
+    for j in range(MB_EARLY, RLOC):
         mb_start(j)
     for c in range(2):
-        @pl.loop(0, RES // 16)
-        def _(j):
-            j0 = pl.multiple_of(j * 16, 16)
-            blk = crecv[pl.ds(j0, 16), 16 * c:16 * c + 16, :].reshape(256, SEQ)
-            cbig[16 * c:16 * c + 16, pl.ds(j0, 16), :] = dot(perm[...], blk).astype(BF16).reshape(16, 16, SEQ)
-
-    @pl.loop(0, OPM // 2)
-    def _(c):
-        prod = dot_t(left[...].reshape(RLOC * OPM, SEQ), cbig[pl.ds(2 * c, 2)].reshape(256, SEQ)).astype(BF16)
-        for u in range(2):
-            outer[:, 2 * c + u] = prod[:, u * LANES:(u + 1) * LANES].reshape(RLOC, OPM, LANES)
-
-    @pl.loop(0, RLOC)
-    def _(i):
-        update = dot(w2t[...], outer[i].reshape(OPM * OPM, LANES))
-        update = update / (1e-3 + norm[pl.ds(me * RLOC + i, 1), :])
-        z1[i] = add_residual(z_ref[i], jnp.transpose(update)[0:RES])
+        for j0 in range(0, RES, 16):
+            blk = crecv[j0:j0 + 16, 16 * c:16 * c + 16, :].reshape(256, SEQ)
+            cbig[16 * c:16 * c + 16, j0:j0 + 16, :] = dot(perm[...], blk).astype(BF16).reshape(16, 16, SEQ)
+
+    @pl.loop(0, OPM // 8)
+    def _(blk):
+        for c2 in range(4):
+            c = blk * 4 + c2
+            prod = dot_t(left[...].reshape(RLOC * OPM, SEQ), cbig[pl.ds(2 * c, 2)].reshape(256, SEQ)).astype(BF16)
+            for u in range(2):
+                outer[:, 2 * c + u] = prod[:, u * LANES:(u + 1) * LANES].reshape(RLOC, OPM, LANES)
+
+    @pl.loop(0, 2)
+    def _(half):
+        for u in range(RLOC // 2):
+            i = half * (RLOC // 2) + u
+            update = dot(w2t[...], outer[i].reshape(OPM * OPM, LANES))
+            update = update / (1e-3 + norm[pl.ds(me * RLOC + i, 1), :])
+            z1[i] = add_residual(z_ref[i], jnp.transpose(update)[0:RES])
 
     def z_src(buf, group):
         return lambda d: buf.at[group, pl.ds(d * RLOC, RLOC)]
@@ -448,17 +447,14 @@
         return lambda s: buf.at[group, s]
 
     def triangle(state, result, w_in, which, w_out, recv, stage, late, send, zrecv, moved, zstage, slot):
-        @pl.loop(0, RLOC)
-        def _(i):
-            ynorm[i, 0:RES, :] = layer_norm(state[i])
+        ynorm[:, 0:RES, :] = layer_norm(state[0:RLOC].reshape(RLOC * RES, CZ)).reshape(RLOC, RES, CZ)
         send_bias(recv, which, HT, stage)
 
-        @pl.loop(0, RLOC // 4)
-        def _(blk):
-            y = ynorm[pl.ds(blk * 4, 4), 0:RES, :].reshape(4 * RES, CZ)
+        for blk in range(RLOC // 4):
+            y = ynorm[blk * 4:blk * 4 + 4, 0:RES, :].reshape(4 * RES, CZ)
             qk = dot(y, w_in[:, 0:2 * CZ]).astype(BF16)
             for t in range(2):
-                triqk[t, pl.ds(blk * 4, 4), 0:RES, :] = qk[:, t * LANES:(t + 1) * LANES].reshape(4, RES, LANES)
+                triqk[t, blk * 4:blk * 4 + 4, 0:RES, :] = qk[:, t * LANES:(t + 1) * LANES].reshape(4, RES, LANES)
         take_bias(recv, HT, stage)
         for j in late:
             mb_start(j)
@@ -481,12 +477,11 @@
             local_copy(z_src(send, group)(me), z_dst(zrecv, group)(me), slot + group).wait()
             wait_recv(zstage + group, z_dst(zrecv, group))
 
-        @pl.loop(0, RLOC)
-        def _(i):
+        for i in range(RLOC):
             rows = zrecv[:, :, i].astype(F32).reshape(LANES, CZ).astype(BF16)
             moved[i] = dot(compz[...], rows).astype(BF16)
 
-    triangle(z1, z1, w_start_in, 1, w_start_out, stb_recv, STB, (MB_EARLY + 3,), zs, zr, z2, ZF, NCHUNK)
+    triangle(z1, z1, w_start_in, 1, w_start_out, stb_recv, STB, (), zs, zr, z2, ZF, NCHUNK)
     triangle(z2, z3, w_end_in, 2, w_end_out, enb_recv, ENB, (), zs2, zr2, z_out, ZB, NCHUNK + 2)
 
     wait_recv(MB, lambda s: mback.at[pl.ds(s * RLOC, RLOC)])

time: 117 us -> 100 us (0.85)
  Pallas kernels: 116 us -> 99.3 us
    pallas_call x1, Pallas kernels: 112 us -> 95.1 us  [per_device(): pl.pallas_call(block_kernel, name='evoformer_block', out_shape=(jax.Shape...]
where the time goes in v8:
time: 100 us
  Pallas kernels  99.3 us (99%)
    pallas_call x1, Pallas kernels, per_device(): pl.pallas_call(block_kernel, name='evoformer_block', out_shape=(jax.Shape...  95.1 us
    pallas_call x1, Pallas kernels, per_device(): pl.pallas_call(finish_kernel, name='finish', grid=(NCHUNK,), out_shape=(j...  4.22 us

profile of v8, /device:TPU:0, one launch (start us, length us, event | category | flops | bytes accessed | tf_op | source)
XLA Modules:
  0.0 100.0 jit_solution(11537829709521860406)
XLA Ops:
  0.6 95.1 %evoformer_block.1 = (bf16[96,4,8,256]{3,2,1,0:T(8,128)(2,1)}, bf16[12,96,128]{2,1,0:T(8,128)(2,1)}) custom-call(bf16[32,96,256]{2,1,0:T(8,128)(2,1)} %m_any.1, bf16[12,96,128]{2,1,0:T(8,128)(2,1)} %z_ref.1, s32[96,256]{1,0:T(8,128)} %bitcast.6, s32[1,96]{1,0:T(1,128)} %bitcast.11, bf16[256,1024]{1,0:T(8,128)(2,1)} %row_in_any.1, bf16[8,128]{1,0:T(8,128)(2,1)} %bitcast.8, ...), custom_call_target="tpu_custom_call" | custom-call | tf_op jit(solution)/shard_map/evoformer_block/pallas_call | solution.py:581
  95.8 4.2 %finish.1 = (bf16[32,96,256]{2,1,0:T(8,128)(2,1)}, bf16[12,96,128]{2,1,0:T(8,128)(2,1)}) custom-call(bf16[96,4,8,256]{3,2,1,0:T(8,128)(2,1)} %get-tuple-element.4.m_home, bf16[12,96,128]{2,1,0:T(8,128)(2,1)} %get-tuple-element.5.z_new), custom_call_target="tpu_custom_call" | custom-call | tf_op jit(solution)/shard_map/finish/pallas_call | solution.py:593

commit v9 on v8

--- a/solution.py
+++ b/solution.py
@@ -36,8 +36,8 @@
 NCHUNK = SLOC // CHUNK
 CROWS = NDEV * CHUNK
 LAG = 4
-MB_EARLY = 10
-NRES = 2
+MB_EARLY = 8
+NRES = 4
 
 
 def dot(a, b):
@@ -289,8 +289,8 @@
             w2[16 * c:16 * c + 16, 16 * a:16 * a + 16, :] = dot(perm[...], blk).astype(BF16).reshape(16, 16, CZ)
     w2t[...] = dot_t(eye, w2[...].reshape(OPM * OPM, CZ)).astype(BF16)
     cbig[:, RES:, :] = jnp.zeros((OPM, LANES - RES, SEQ), BF16)
-    yrow[:, RES:, :] = jnp.zeros((4, LANES - RES, CM), BF16)
-    rowqk[:, :, RES:, :] = jnp.zeros((4, 4, LANES - RES, LANES), BF16)
+    yrow[:, RES:, :] = jnp.zeros((CHUNK, LANES - RES, CM), BF16)
+    rowqk[:, :, RES:, :] = jnp.zeros((4, CHUNK, LANES - RES, LANES), BF16)
     triqk[:, :, RES:, :] = jnp.zeros((2, RLOC, LANES - RES, LANES), BF16)
     z1[RLOC:, :, :] = jnp.zeros((16 - RLOC, RES, CZ), BF16)
     z3[...] = jnp.zeros_like(z3)
@@ -307,21 +307,20 @@
         return pltpu.make_async_copy(src, dst, local_sem.at[n])
 
     def row_chunk(q):
-        @pl.loop(0, CHUNK // 4)
-        def _(blk):
-            s0 = q * CHUNK + blk * 4
-            x = m_ref[pl.ds(s0, 4)].reshape(4 * RES, CM)
-            y = layer_norm(x)
-            yrow[:, 0:RES, :] = y.reshape(4, RES, CM)
+        s0 = q * CHUNK
+        for part in range(CHUNK // 4):
+            here = slice(4 * part, 4 * part + 4)
+            y = layer_norm(m_ref[s0 + 4 * part:s0 + 4 * part + 4].reshape(4 * RES, CM))
+            yrow[here, 0:RES, :] = y.reshape(4, RES, CM)
             qk = dot(y, w_row_in[:, 0:2 * CM]).astype(BF16)
             for t in range(4):
-                rowqk[t, :, 0:RES, :] = qk[:, t * LANES:(t + 1) * LANES].reshape(4, RES, LANES)
-
-            def store(u, update):
-                m1[s0 + u] = add_residual(m_ref[s0 + u], update[0:RES])
-            attend_biased(range(4), 2, lambda u, t: rowqk[t, u], lambda u, t: rowqk[2 + t, u, 0:RES],
-                          lambda u: dot_t(row_vg[...], yrow[u]).astype(BF16), bias,
-                          lambda u: keep_row[s0 + u], w_row_out[...], store)
+                rowqk[t, here, 0:RES, :] = qk[:, t * LANES:(t + 1) * LANES].reshape(4, RES, LANES)
+
+        def store(u, update):
+            m1[s0 + u] = add_residual(m_ref[s0 + u], update[0:RES])
+        attend_biased(range(CHUNK), 2, lambda u, t: rowqk[t, u], lambda u, t: rowqk[2 + t, u, 0:RES],
+                      lambda u: dot_t(row_vg[...], yrow[u]).astype(BF16), bias,
+                      lambda u: keep_row[s0 + u], w_row_out[...], store)
 
         for j in range(RES // 32):
             blk = m1[CHUNK * q:CHUNK * q + CHUNK, 32 * j:32 * j + 32, :].reshape(256, CM)
@@ -543,8 +542,8 @@
             pltpu.VMEM((2 * CM, CM), BF16),
             pltpu.VMEM((2 * CM, CM), BF16),
             pltpu.VMEM((2, 2 * CZ, CZ), BF16),
-            pltpu.VMEM((4, LANES, CM), BF16),
-            pltpu.VMEM((4, 4, LANES, LANES), BF16),
+            pltpu.VMEM((CHUNK, LANES, CM), BF16),
+            pltpu.VMEM((4, CHUNK, LANES, LANES), BF16),
             pltpu.VMEM((2, RLOC, LANES, LANES), BF16),
             pltpu.VMEM((SLOC, RES, CM), BF16),
             pltpu.VMEM((NCHUNK, RES, CHUNK, CM), BF16),

time: 100 us -> 101 us (1.010)
  no operation moved by 1% of the time
where the time goes in v9:
time: 101 us
  Pallas kernels  99.9 us (99%)
    pallas_call x1, Pallas kernels, per_device(): pl.pallas_call(block_kernel, name='evoformer_block', out_shape=(jax.Shape...  95.7 us
    pallas_call x1, Pallas kernels, per_device(): pl.pallas_call(finish_kernel, name='finish', grid=(NCHUNK,), out_shape=(j...  4.22 us

profile of v9, /device:TPU:0, one launch (start us, length us, event | category | flops | bytes accessed | tf_op | source)
XLA Modules:
  0.0 100.5 jit_solution(13730118941607187190)
XLA Ops:
  0.6 95.7 %evoformer_block.1 = (bf16[96,4,8,256]{3,2,1,0:T(8,128)(2,1)}, bf16[12,96,128]{2,1,0:T(8,128)(2,1)}) custom-call(bf16[32,96,256]{2,1,0:T(8,128)(2,1)} %m_any.1, bf16[12,96,128]{2,1,0:T(8,128)(2,1)} %z_ref.1, s32[96,256]{1,0:T(8,128)} %bitcast.6, s32[1,96]{1,0:T(1,128)} %bitcast.11, bf16[256,1024]{1,0:T(8,128)(2,1)} %row_in_any.1, bf16[8,128]{1,0:T(8,128)(2,1)} %bitcast.8, ...), custom_call_target="tpu_custom_call" | custom-call | tf_op jit(solution)/shard_map/evoformer_block/pallas_call | solution.py:580
  96.3 4.2 %finish.1 = (bf16[32,96,256]{2,1,0:T(8,128)(2,1)}, bf16[12,96,128]{2,1,0:T(8,128)(2,1)}) custom-call(bf16[96,4,8,256]{3,2,1,0:T(8,128)(2,1)} %get-tuple-element.4.m_home, bf16[12,96,128]{2,1,0:T(8,128)(2,1)} %get-tuple-element.5.z_new), custom_call_target="tpu_custom_call" | custom-call | tf_op jit(solution)/shard_map/finish/pallas_call | solution.py:592

commit v10 on v9

--- a/solution.py
+++ b/solution.py
@@ -36,7 +36,6 @@
 NCHUNK = SLOC // CHUNK
 CROWS = NDEV * CHUNK
 LAG = 4
-MB_EARLY = 8
 NRES = 4
 
 
@@ -385,25 +384,23 @@
             done = x.astype(F32).reshape(NCHUNK, NDEV, CHUNK, CM).astype(BF16)
             for d in range(NDEV):
                 mdone[d, j] = done[:, d]
-
-        attend_column(range(NRES), lambda u, t: colqk[t, pair * NRES + u], lambda u, t: ckeep[u, t], lambda u: caug[u],
-                      ones[0:LANES], lambda u: dot_t(col_vg[...], ycol[pair * NRES + u]).astype(BF16), w_col_out[...], store)
-        for u in range(NRES):
-            j = pair * NRES + u
             row = crecv.at[me * RLOC + j]
             for t, twin in enumerate(twins):
                 remote(row, row, c_send.at[t], c_recv.at[t, j], twin).start()
             remote(row, row, c_send.at[6], c_pair.at[3], partner).start()
-
+            if u < NRES - 1:
+                mb_start(j)
+
+        attend_column(range(NRES), lambda u, t: colqk[t, pair * NRES + u], lambda u, t: ckeep[u, t], lambda u: caug[u],
+                      ones[0:LANES], lambda u: dot_t(col_vg[...], ycol[pair * NRES + u]).astype(BF16), w_col_out[...], store)
         @pl.when(pair >= LAG // NRES)
         def _():
             for u in range(NRES):
                 relay(pair * NRES - LAG + u)
 
-        @pl.when(pair < MB_EARLY // NRES)
+        @pl.when(pair < RLOC // NRES - 1)
         def _():
-            for u in range(NRES):
-                mb_start(pair * NRES + u)
+            mb_start(pair * NRES + NRES - 1)
 
     for j in range(RLOC - LAG, RLOC):
         relay(j)
@@ -416,8 +413,7 @@
     for t, first in enumerate(twins + (me,)):
         rows = c_rows(first + 1 - 2 * core)
         remote(rows, rows, c_send.at[3 + t], c_pair.at[t], partner).wait_recv()
-    for j in range(MB_EARLY, RLOC):
-        mb_start(j)
+    mb_start(RLOC - 1)
     for c in range(2):
         for j0 in range(0, RES, 16):
             blk = crecv[j0:j0 + 16, 16 * c:16 * c + 16, :].reshape(256, SEQ)

time: 101 us -> 99.3 us (0.983)
  Pallas kernels: 99.9 us -> 98.5 us
    pallas_call x1, Pallas kernels: 95.7 us -> 94.3 us  [per_device(): pl.pallas_call(block_kernel, name='evoformer_block', out_shape=(jax.Shape...]
where the time goes in v10:
time: 99.3 us; the launch traced here: 99.2 us
  Pallas kernels  98.5 us (99%)
    pallas_call x1, Pallas kernels, per_device(): pl.pallas_call(block_kernel, name='evoformer_block', out_shape=(jax.Shape...  94.3 us
    pallas_call x1, Pallas kernels, per_device(): pl.pallas_call(finish_kernel, name='finish', grid=(NCHUNK,), out_shape=(j...  4.22 us

profile of v10, /device:TPU:0, one launch (start us, length us, event | category | flops | bytes accessed | tf_op | source)
XLA Modules:
  0.0 99.2 jit_solution(6391994808651558730)
XLA Ops:
  0.6 94.3 %evoformer_block.1 = (bf16[96,4,8,256]{3,2,1,0:T(8,128)(2,1)}, bf16[12,96,128]{2,1,0:T(8,128)(2,1)}) custom-call(bf16[32,96,256]{2,1,0:T(8,128)(2,1)} %m_any.1, bf16[12,96,128]{2,1,0:T(8,128)(2,1)} %z_ref.1, s32[96,256]{1,0:T(8,128)} %bitcast.6, s32[1,96]{1,0:T(1,128)} %bitcast.11, bf16[256,1024]{1,0:T(8,128)(2,1)} %row_in_any.1, bf16[8,128]{1,0:T(8,128)(2,1)} %bitcast.8, ...), custom_call_target="tpu_custom_call" | custom-call | tf_op jit(solution)/shard_map/evoformer_block/pallas_call | solution.py:576
  94.9 4.2 %finish.1 = (bf16[32,96,256]{2,1,0:T(8,128)(2,1)}, bf16[12,96,128]{2,1,0:T(8,128)(2,1)}) custom-call(bf16[96,4,8,256]{3,2,1,0:T(8,128)(2,1)} %get-tuple-element.4.m_home, bf16[12,96,128]{2,1,0:T(8,128)(2,1)} %get-tuple-element.5.z_new), custom_call_target="tpu_custom_call" | custom-call | tf_op jit(solution)/shard_map/finish/pallas_call | solution.py:588
